TPU v7x, 32 devices: a whole 2x2x4 slice. The times are simulated.
32 devices in a mesh: gx: 8 (over z, x), gy: 4 (over y, core).
Axes of the slice: x: 2, y: 2, z: 4, core: 2. Of those that a mesh axis runs over, the one named last changes fastest.
Arguments:
- populations: float32 [19, 64, 256, 256], P(None, 'gx', 'gy'), may hold values from 0 to 0.6
- rotation_init: float32 [3], replicated, may hold values from -0.75 to 0.75
- slot_cell: int32 [3, 8, 4, 2048], P(None, 'gx', 'gy'), may hold values from 0 to 255, as said below
- slot_count: int32 [8, 4], P('gx', 'gy'), may hold values from 128 to 2048, as said below
- marker_arm: float32 [3, 8, 4, 2048], P(None, 'gx', 'gy'), may hold values from -1.7 to 1.7
- marker_area: float32 [8, 4, 2048], P('gx', 'gy'), may hold values from 0.3 to 3
- marker_fraction: float32 [8, 4, 2048], P('gx', 'gy'), may hold values from 0 to 1
Outputs:
- populations_next: float32 [19, 64, 256, 256], P(None, 'gx', 'gy')
- rotation: float32 [3, 3], replicated
Inputs may be any that keep to these rules, and one draw needn't show every extreme that they name: `slot_cell`: slot s of slab (a, b) names a cell whose first coordinate lies in [a * 8, (a + 1) * 8) and whose second lies in [b * 64, (b + 1) * 64); the third is any; slots at or past slot_count hold cells too but carry no marker. `slot_count`: some slab has all 2048 slots live in every draw.
All inputs are finite; a program needn't handle non-finite values.
Results may differ from a plain program's by a relative error of at most 0.0001.
Values sent between devices are 32-bit elements; how exact they have to be, the bound alone decides.
A program may use at most 128 MiB of HBM per device.

v0:
```python
import functools

import jax
import jax.numpy as jnp
from jax import lax
from jax.experimental import pallas as pl
from jax.experimental.pallas import tpu as pltpu
from jax.sharding import PartitionSpec as P

Q = 19
ITERS = 3
VELOCITY_TABLE = (
    (0, 0, 0),
    (1, 0, 0),
    (-1, 0, 0),
    (0, 1, 0),
    (0, -1, 0),
    (0, 0, 1),
    (0, 0, -1),
    (1, 1, 0),
    (-1, -1, 0),
    (1, -1, 0),
    (-1, 1, 0),
    (1, 0, 1),
    (-1, 0, -1),
    (1, 0, -1),
    (-1, 0, 1),
    (0, 1, 1),
    (0, -1, -1),
    (0, 1, -1),
    (0, -1, 1),
)
WEIGHT_TABLE = (1.0 / 3.0,) + (1.0 / 18.0,) * 6 + (1.0 / 36.0,) * 12
RELAX_TIME = 0.8
SPREAD_GAIN = 0.25
SPIN_GAIN = 0.5
PLUS_X = [m for m in range(Q) if VELOCITY_TABLE[m][0] == 1]
MINUS_X = [m for m in range(Q) if VELOCITY_TABLE[m][0] == -1]
PLUS_Y = [m for m in range(Q) if VELOCITY_TABLE[m][1] == 1]
MINUS_Y = [m for m in range(Q) if VELOCITY_TABLE[m][1] == -1]
DIAGONAL = [m for m in range(Q) if VELOCITY_TABLE[m][0] != 0 and VELOCITY_TABLE[m][1] != 0]
MESH = pl.DeviceIdType.MESH
F32 = jnp.float32
BF16 = jnp.bfloat16
VMEM = pltpu.VMEM
VMEM_LIMIT = 60 * 1024 * 1024


def vmem():
    return pl.BlockSpec(memory_space=pltpu.VMEM)


def relax(member, value, density, velocity, common):
    direction = VELOCITY_TABLE[member]
    projected = None
    for number in range(3):
        if direction[number] != 0:
            term = velocity[number] if direction[number] > 0 else -velocity[number]
            projected = term if projected is None else projected + term
    scaled = density * (WEIGHT_TABLE[member] / RELAX_TIME)
    if projected is None:
        bracket = common
    else:
        bracket = common + projected * (3.0 + 4.5 * projected)
    return value * (1.0 - 1.0 / RELAX_TIME) + scaled * bracket


def common_of(velocity):
    squared = velocity[0] * velocity[0] + velocity[1] * velocity[1] + velocity[2] * velocity[2]
    return 1.0 - 1.5 * squared


def moments_kernel(pops_ref, density_ref, velocity_ref, held, sems):
    layers, size_y, depth = pops_ref.shape[1], pops_ref.shape[2], pops_ref.shape[3]

    def incoming(layer):
        return pltpu.make_async_copy(pops_ref.at[:, layer], held.at[layer], sems.at[layer])

    for layer in range(layers):
        incoming(layer).start()

    def one(layer, carry):
        incoming(layer).wait()
        at = pl.ds(pl.multiple_of(layer * size_y, size_y), size_y)
        values = [held[layer, m] for m in range(Q)]
        density = values[0]
        for m in range(1, Q):
            density = density + values[m]
        density_ref[at, :] = density
        for number in range(3):
            total = None
            for m in range(Q):
                direction = VELOCITY_TABLE[m][number]
                if direction != 0:
                    if total is None:
                        total = values[m]
                    else:
                        total = total + values[m] if direction > 0 else total - values[m]
            velocity_ref[at, number * depth : (number + 1) * depth] = total / density
        return carry

    lax.fori_loop(0, layers, one, 0)


def pieces_of(value, count):
    found = []
    for number in range(count):
        piece = value.astype(BF16)
        found.append(piece)
        if number < count - 1:
            value = value - piece.astype(F32)
    return found


def depth_table(depth, low, fraction):
    high = jnp.where(low == depth - 1.0, 0.0, low + 1.0)
    ids = lax.broadcasted_iota(jnp.int32, (depth, low.shape[1]), 0).astype(F32)
    return jnp.where(ids == low, 1.0 - fraction, 0.0) + jnp.where(ids == high, fraction, 0.0)


def plane_table(planes, row):
    ids = lax.broadcasted_iota(jnp.int32, (planes, row.shape[1]), 0).astype(F32)
    return jnp.where(ids == row, 1.0, 0.0).astype(BF16)


def gather_kernel(
    velocity_ref,
    pack_ref,
    sums_ref,
    linear_ref,
    turned_hi,
    turned_lo,
    state_ref,
    result_ref,
    cell_col,
    high_col,
    same_ref,
    after_ref,
    before_ref,
    left_ref,
):
    planes, triple = velocity_ref.shape
    depth = triple // 3
    slots = pack_ref.shape[1]
    turned = jnp.transpose(velocity_ref[...])
    hi, lo = pieces_of(turned, 2)
    turned_hi[...] = hi
    turned_lo[...] = lo
    chunk = 512
    steps = slots // chunk

    def gather(step, carry):
        at = pl.ds(pl.multiple_of(step * chunk, chunk), chunk)
        table = plane_table(planes, pack_ref[0:1, at])
        rows = jnp.dot(turned_hi[...], table, preferred_element_type=F32)
        rows = rows + jnp.dot(turned_lo[...], table, preferred_element_type=F32)
        tap = depth_table(depth, pack_ref[1:2, at], pack_ref[3:4, at])
        for number in range(3):
            part = rows[number * depth : (number + 1) * depth]
            state_ref[number : number + 1, at] = jnp.sum(part * tap, axis=0, keepdims=True)
        return carry

    lax.fori_loop(0, steps, gather, 0)
    state_ref[3:6, :] = pack_ref[4:7, :]
    state_ref[6:8, :] = jnp.zeros((2, slots), F32)

    low = pack_ref[1:2, :]
    high = jnp.where(low == depth - 1.0, 0.0, low + 1.0)
    base = pack_ref[0:1, :] * float(depth)
    cell_row = base + low
    high_row = base + high
    both = jnp.concatenate([cell_row, high_row, jnp.zeros((6, slots), F32)], axis=0)
    columns = jnp.transpose(both)
    cell_col[...] = jnp.broadcast_to(columns[:, 0:1], (slots, 128))
    high_col[...] = jnp.broadcast_to(columns[:, 1:2], (slots, 128))
    result_ref[6:8, :] = both[0:2]

    def prepare():
        weighted = state_ref[...] * pack_ref[2:3, :]
        share = pack_ref[3:4, :]
        stacked = jnp.concatenate([weighted * (1.0 - share), weighted * share], axis=0)
        left_ref[...] = jnp.concatenate(pieces_of(stacked, 3), axis=0)

    def apply(build):
        def one(step, carry):
            at = pl.ds(pl.multiple_of(step * chunk, chunk), chunk)
            if build:
                for half in range(chunk // 128):
                    part = pl.ds(pl.multiple_of(step * chunk + half * 128, 128), 128)
                    lanes = slice(half * 128, (half + 1) * 128)
                    cell = result_ref[6:7, part]
                    cell_high = result_ref[7:8, part]
                    same_ref[step, :, lanes] = jnp.where(cell_col[...] == cell, 1.0, 0.0).astype(BF16)
                    after_ref[step, :, lanes] = jnp.where(high_col[...] == cell, 1.0, 0.0).astype(BF16)
                    before_ref[step, :, lanes] = jnp.where(cell_col[...] == cell_high, 1.0, 0.0).astype(BF16)
            left = left_ref[...]

            def product(table):
                out = jnp.dot(left, table, preferred_element_type=F32)
                return out[0:16] + out[16:32] + out[32:48]

            same = product(same_ref[step])
            after = product(after_ref[step])
            before = product(before_ref[step])
            share = pack_ref[3:4, at]
            total = (1.0 - share) * (same[0:8] + after[8:16]) + share * (same[8:16] + before[0:8])
            result_ref[0:6, at] = SPREAD_GAIN * total[0:6]
            return carry

        lax.fori_loop(0, steps, one, 0)

    prepare()
    apply(True)
    arm = pack_ref[4:7, :]
    weight = pack_ref[2:3, :]
    first = state_ref[0:3, :]
    second = first - result_ref[0:3, :]
    carried = result_ref[3:6, :]
    state_ref[0:3, :] = second
    state_ref[3:6, :] = carried
    prepare()
    apply(False)
    third = second - result_ref[0:3, :]
    later = carried - result_ref[3:6, :]
    heavy = arm * weight
    rows = []
    for vector in (arm, carried, later):
        for a in range(3):
            rows.append(heavy[a : a + 1] * vector)
    for vector in (first, second, third):
        rows.append(heavy[1:2] * vector[2:3] - heavy[2:3] * vector[1:2])
        rows.append(heavy[2:3] * vector[0:1] - heavy[0:1] * vector[2:3])
        rows.append(heavy[0:1] * vector[1:2] - heavy[1:2] * vector[0:1])
    rows.append(jnp.zeros((4, slots), F32))
    table = jnp.concatenate(rows, axis=0)
    column = jnp.broadcast_to(jnp.sum(table, axis=1, keepdims=True), (40, 128))
    square = jnp.concatenate([column, jnp.zeros((88, 128), F32)], axis=0)
    sums_ref[...] = jnp.transpose(square)[0:8]
    linear_ref[0:3, :] = heavy
    linear_ref[3:6, :] = weight * (first + second + third)
    linear_ref[6:9, :] = weight * (carried + later)
    linear_ref[9:12, :] = weight * carried
    linear_ref[12:16, :] = jnp.zeros((4, slots), F32)


def total_kernel(x_count, y_count, part_ref, out_ref, near, mine, far, near_send, near_recv, far_send, far_recv):
    x = lax.axis_index("gx")
    y = lax.axis_index("gy")
    barrier = pltpu.get_barrier_semaphore()
    for step in range(1, y_count):
        pl.semaphore_signal(barrier, inc=1, device_id=(x, lax.rem(y + step, y_count)), device_id_type=MESH)
    for step in range(1, x_count):
        pl.semaphore_signal(barrier, inc=1, device_id=(lax.rem(x + step, x_count), y), device_id_type=MESH)
    pl.semaphore_wait(barrier, x_count + y_count - 2)

    def near_copy(step):
        return pltpu.make_async_remote_copy(
            src_ref=part_ref,
            dst_ref=near.at[step - 1],
            send_sem=near_send.at[step - 1],
            recv_sem=near_recv.at[step - 1],
            device_id=(x, lax.rem(y + step, y_count)),
            device_id_type=MESH,
        )

    def far_copy(step):
        return pltpu.make_async_remote_copy(
            src_ref=mine,
            dst_ref=far.at[step - 1],
            send_sem=far_send.at[step - 1],
            recv_sem=far_recv.at[step - 1],
            device_id=(lax.rem(x + step, x_count), y),
            device_id_type=MESH,
        )

    def ordered(own, slots, count, position):
        total = None
        for source in range(count):
            value = own
            for step in range(1, count):
                hit = lax.rem(position + count - step, count) == source
                value = jnp.where(hit, slots[step - 1], value)
            total = value if total is None else total + value
        return total

    for step in range(1, y_count):
        near_copy(step).start()
    for step in range(1, y_count):
        near_copy(step).wait()
    mine[...] = ordered(part_ref[...], near, y_count, y)
    for step in range(1, x_count):
        far_copy(step).start()
    for step in range(1, x_count):
        far_copy(step).wait()
    out_ref[...] = ordered(mine[...], far, x_count, x)


def cross(first, second):
    return [
        first[1] * second[2] - first[2] * second[1],
        first[2] * second[0] - first[0] * second[2],
        first[0] * second[1] - first[1] * second[0],
    ]


def spread_kernel(
    rows_y,
    spin_ref,
    sums_ref,
    linear_ref,
    pack_ref,
    velocity_ref,
    density_ref,
    pops_ref,
    moved_ref,
    spins_ref,
    x_up_ref,
    x_down_ref,
    y_up_ref,
    y_down_ref,
    corner_a,
    corner_b,
    corner_c,
    corner_d,
    table_ref,
    hi_ref,
    lo_ref,
    x_in,
    y_in,
    turned,
    x_sem,
    y_sem,
):
    planes, depth = density_ref.shape
    rows_x = planes // rows_y
    copies = []
    for number, m in enumerate(PLUS_X + MINUS_X):
        layer = rows_x - 1 if m in PLUS_X else 0
        copies.append(pltpu.make_async_copy(pops_ref.at[m, layer], x_in.at[number], x_sem.at[number]))
    for number, m in enumerate(PLUS_Y + MINUS_Y):
        row = rows_y - 1 if m in PLUS_Y else 0
        copies.append(pltpu.make_async_copy(pops_ref.at[m, :, row], y_in.at[number], y_sem.at[number]))
    for copy in copies:
        copy.start()

    turned[...] = jnp.transpose(jnp.broadcast_to(sums_ref[0:1, :], (128, 128)))

    def number_at(index):
        return turned[index : index + 1, 0:1]

    def turning(offset, spin):
        entry = [[number_at(offset + a * 3 + b) for b in range(3)] for a in range(3)]
        trace = entry[0][0] + entry[1][1] + entry[2][2]
        return [
            spin[b] * trace - (entry[0][b] * spin[0] + entry[1][b] * spin[1] + entry[2][b] * spin[2])
            for b in range(3)
        ]

    inertia = number_at(0) + number_at(4) + number_at(8)
    spin = [spin_ref[0:1, number : number + 1] for number in range(3)]
    spins = [spin]
    for step in range(ITERS):
        own = turning(0, spins[step])
        torque = [number_at(27 + step * 3 + b) - own[b] for b in range(3)]
        if step >= 1:
            back = turning(9, spins[step - 1])
            torque = [torque[b] + back[b] for b in range(3)]
        if step >= 2:
            back = turning(18, spins[step - 2])
            torque = [torque[b] + back[b] for b in range(3)]
        spins.append([spins[step][b] + SPIN_GAIN * torque[b] / inertia for b in range(3)])
        for b in range(3):
            spins_ref[step : step + 1, b : b + 1] = spins[step + 1][b]
    whole = [spins[0][b] + spins[1][b] + spins[2][b] for b in range(3)]

    def linear(start):
        return [linear_ref[start + b : start + b + 1, :] for b in range(3)]

    lead = cross(whole, linear(0))
    fall = linear(3)
    zeroth = cross(spins[0], linear(6))
    once = cross(spins[1], linear(9))
    impulse = [SPREAD_GAIN * (lead[b] - fall[b] - zeroth[b] - once[b]) for b in range(3)]
    table_ref[...] = plane_table(planes, pack_ref[0:1, :])
    tap = depth_table(depth, pack_ref[1:2, :], pack_ref[3:4, :])
    for number in range(3):
        lanes = slice(number * depth, (number + 1) * depth)
        hi, lo = pieces_of(tap * impulse[number], 2)
        hi_ref[lanes, :] = hi
        lo_ref[lanes, :] = lo
    dims = (((1,), (1,)), ((), ()))
    added = lax.dot_general(table_ref[...], hi_ref[...], dims, preferred_element_type=F32)
    added = added + lax.dot_general(table_ref[...], lo_ref[...], dims, preferred_element_type=F32)
    moved_ref[...] = velocity_ref[...] + added

    for copy in copies:
        copy.wait()

    def face(at, members, incoming, first):
        velocity = [moved_ref[at, number * depth : (number + 1) * depth] for number in range(3)]
        common = common_of(velocity)
        density = density_ref[at, :]
        return [
            relax(m, incoming[first + index], density, velocity, common)
            for index, m in enumerate(members)
        ]

    corners = {7: corner_a, 8: corner_b, 9: corner_c, 10: corner_d}
    for members, out, layer, first in (
        (PLUS_X, x_up_ref, rows_x - 1, 0),
        (MINUS_X, x_down_ref, 0, len(PLUS_X)),
    ):
        found = face(pl.ds(layer * rows_y, rows_y), members, x_in, first)
        for index, m in enumerate(members):
            out[index] = found[index]
            if m in DIAGONAL:
                row = rows_y - 1 if VELOCITY_TABLE[m][1] == 1 else 0
                corners[m][...] = found[index][row : row + 1]
    for members, out, row, first in (
        (PLUS_Y, y_up_ref, rows_y - 1, 0),
        (MINUS_Y, y_down_ref, 0, len(PLUS_Y)),
    ):
        def strided(ref, lanes):
            return jnp.concatenate(
                [ref[x * rows_y + row : x * rows_y + row + 1, lanes] for x in range(rows_x)], axis=0
            )

        velocity = [strided(moved_ref, slice(n * depth, (n + 1) * depth)) for n in range(3)]
        density = strided(density_ref, slice(0, depth))
        common = common_of(velocity)
        for index, m in enumerate(members):
            out[index] = relax(m, y_in[first + index], density, velocity, common)


def roll(value, steps, axis):
    if steps == 0:
        return value
    return pltpu.roll(value, steps % value.shape[axis], axis)


def collide_kernel(layers, pops_ref, velocity_ref, density_ref, out_ref, held, speed, mass, in_sems, sems):
    size_y, depth = held.shape[2], held.shape[3]

    def incoming(layer):
        rows = pl.ds(pl.multiple_of(layer * size_y, size_y), size_y)
        return [
            pltpu.make_async_copy(pops_ref.at[:, layer], held.at[layer], in_sems.at[0, layer]),
            pltpu.make_async_copy(velocity_ref.at[rows], speed.at[layer], in_sems.at[1, layer]),
            pltpu.make_async_copy(density_ref.at[rows], mass.at[layer], in_sems.at[2, layer]),
        ]

    def outgoing(layer, action):
        for m in range(Q):
            step = VELOCITY_TABLE[m][0]

            def go(m=m, step=step):
                copy = pltpu.make_async_copy(held.at[layer, m], out_ref.at[m, layer + step], sems.at[layer, m])
                copy.start() if action == "start" else copy.wait()

            if step == 0:
                go()
            elif step == 1:
                pl.when(layer < layers - 1)(go)
            else:
                pl.when(layer > 0)(go)

    for layer in range(layers):
        for copy in incoming(layer):
            copy.start()

    def one(layer, carry):
        for copy in incoming(layer):
            copy.wait()
        velocity = [speed[layer, :, n * depth : (n + 1) * depth] for n in range(3)]
        density = mass[layer]
        common = common_of(velocity)
        for m in range(Q):
            value = relax(m, held[layer, m], density, velocity, common)
            value = roll(roll(value, VELOCITY_TABLE[m][1], 0), VELOCITY_TABLE[m][2], 1)
            held[layer, m] = value
        outgoing(layer, "start")
        return carry

    lax.fori_loop(0, layers, one, 0)

    def finish(layer, carry):
        outgoing(layer, "wait")
        return carry

    lax.fori_loop(0, layers, finish, 0)


def trade_kernel(x_count, y_count, *refs):
    ways = ((0, 1), (0, -1), (1, 1), (-1, -1), (1, -1), (-1, 1))
    count = len(ways)
    sources = refs[:count]
    targets, slots = refs[count + 1 : 2 * count + 1], refs[2 * count + 1 : 3 * count + 1]
    send_sem, recv_sem = refs[3 * count + 1 :]
    x = lax.axis_index("gx")
    y = lax.axis_index("gy")
    others = [(lax.rem(x + dx + x_count, x_count), lax.rem(y + dy + y_count, y_count)) for dx, dy in ways]
    barrier = pltpu.get_barrier_semaphore()
    for other in others:
        pl.semaphore_signal(barrier, inc=1, device_id=other, device_id_type=MESH)
    pl.semaphore_wait(barrier, count)
    copies = [
        pltpu.make_async_remote_copy(
            src_ref=sources[n],
            dst_ref=slots[n],
            send_sem=send_sem.at[n],
            recv_sem=recv_sem.at[n],
            device_id=others[n],
            device_id_type=MESH,
        )
        for n in range(count)
    ]
    for copy in copies:
        copy.start()
    for copy in copies:
        copy.wait()
    for n in range(count):
        targets[n][...] = slots[n][...]


def edge_kernel(whole_ref, x_low, x_high, y_low, y_high, ca, cb, cc, cd, out_ref, face, strip, face_sem, strip_sem):
    del whole_ref
    layers, rows_y = out_ref.shape[1], out_ref.shape[2]
    corners = {7: ca, 8: cb, 9: cc, 10: cd}
    copies = []
    number = 0
    for members, source, layer in ((PLUS_X, x_low, 0), (MINUS_X, x_high, layers - 1)):
        for index, m in enumerate(members):
            step_y, step_z = VELOCITY_TABLE[m][1], VELOCITY_TABLE[m][2]
            value = source[index]
            if step_y == 1:
                value = jnp.concatenate([corners[m][...], value[: rows_y - 1]], axis=0)
            elif step_y == -1:
                value = jnp.concatenate([value[1:], corners[m][...]], axis=0)
            face[number] = roll(value, step_z, 1)
            copies.append(pltpu.make_async_copy(face.at[number], out_ref.at[m, layer], face_sem.at[number]))
            number += 1
    number = 0
    for members, source, row in ((PLUS_Y, y_low, 0), (MINUS_Y, y_high, rows_y - 1)):
        for index, m in enumerate(members):
            step_x, step_z = VELOCITY_TABLE[m][0], VELOCITY_TABLE[m][2]
            strip[number] = roll(source[index], step_z, 1)
            count = layers - abs(step_x)
            source_at = 1 if step_x == -1 else 0
            target_at = 1 if step_x == 1 else 0
            copies.append(
                pltpu.make_async_copy(
                    strip.at[number, pl.ds(source_at, count)],
                    out_ref.at[m, pl.ds(target_at, count), row],
                    strip_sem.at[number],
                )
            )
            number += 1
    for copy in copies:
        copy.start()
    for copy in copies:
        copy.wait()


def shifted(value, steps_x, steps_y):
    count_x, count_y = lax.axis_size("gx"), lax.axis_size("gy")
    pairs = []
    for x in range(count_x):
        for y in range(count_y):
            target = ((x + steps_x) % count_x) * count_y + (y + steps_y) % count_y
            pairs.append((x * count_y + y, target))
    return lax.ppermute(value, ("gx", "gy"), pairs)


def local(
    populations, rotation_init, slot_cell, slot_count, marker_arm, marker_area, marker_fraction
):
    _, size_x, size_y, depth = populations.shape
    slots = marker_area.shape[2]
    planes = size_x * size_y
    shape = jax.ShapeDtypeStruct
    params = pltpu.CompilerParams(vmem_limit_bytes=VMEM_LIMIT)
    cell = slot_cell.reshape(3, slots)
    plane = (cell[0] - lax.axis_index("gx") * size_x) * size_y + cell[1] - lax.axis_index("gy") * size_y
    active = lax.broadcasted_iota(jnp.int32, (slots,), 0) < slot_count.reshape(())
    weight = jnp.where(active, marker_area.reshape(-1), 0.0)
    pack = jnp.concatenate(
        [
            plane.astype(F32)[None],
            cell[2].astype(F32)[None],
            weight[None],
            marker_fraction.reshape(1, slots),
            marker_arm.reshape(3, slots),
            jnp.zeros((1, slots), F32),
        ],
        axis=0,
    )
    held = VMEM((size_x, Q, size_y, depth), F32)
    density, velocity = pl.pallas_call(
        moments_kernel,
        in_specs=[pl.BlockSpec(memory_space=pl.ANY)],
        out_specs=[vmem(), vmem()],
        out_shape=[shape((planes, depth), F32), shape((planes, 3 * depth), F32)],
        scratch_shapes=[held, pltpu.SemaphoreType.DMA((size_x,))],
        compiler_params=params,
        name="moments",
    )(populations)
    table = VMEM((slots // 512, slots, 512), BF16)
    sums, linear = pl.pallas_call(
        gather_kernel,
        in_specs=[vmem()] * 2,
        out_specs=[vmem()] * 2,
        out_shape=[shape((8, 128), F32), shape((16, slots), F32)],
        scratch_shapes=[
            VMEM((3 * depth, planes), BF16),
            VMEM((3 * depth, planes), BF16),
            VMEM((8, slots), F32),
            VMEM((8, slots), F32),
            VMEM((slots, 128), F32),
            VMEM((slots, 128), F32),
            table,
            table,
            table,
            VMEM((48, slots), BF16),
        ],
        compiler_params=params,
        name="gather",
    )(velocity, pack)
    count_x, count_y = lax.axis_size("gx"), lax.axis_size("gy")
    dma = pltpu.SemaphoreType.DMA
    sums = pl.pallas_call(
        functools.partial(total_kernel, count_x, count_y),
        in_specs=[vmem()],
        out_specs=vmem(),
        out_shape=shape((8, 128), F32),
        scratch_shapes=[
            VMEM((count_y - 1, 8, 128), F32),
            VMEM((8, 128), F32),
            VMEM((count_x - 1, 8, 128), F32),
            dma((count_y - 1,)),
            dma((count_y - 1,)),
            dma((count_x - 1,)),
            dma((count_x - 1,)),
        ],
        compiler_params=pltpu.CompilerParams(collective_id=0, has_side_effects=True),
        name="total",
    )(sums)
    x_face = shape((len(PLUS_X), size_y, depth), F32)
    y_face = shape((len(PLUS_Y), size_x, depth), F32)
    corner = shape((1, depth), F32)
    moved, spins, x_up, x_down, y_up, y_down, c7, c8, c9, c10 = pl.pallas_call(
        functools.partial(spread_kernel, size_y),
        in_specs=[vmem()] * 6 + [pl.BlockSpec(memory_space=pl.ANY)],
        out_specs=[vmem()] * 10,
        out_shape=[
            shape((planes, 3 * depth), F32),
            shape((ITERS, 3), F32),
            x_face,
            x_face,
            y_face,
            y_face,
            corner,
            corner,
            corner,
            corner,
        ],
        scratch_shapes=[
            VMEM((planes, slots), BF16),
            VMEM((3 * depth, slots), BF16),
            VMEM((3 * depth, slots), BF16),
            VMEM((2 * len(PLUS_X), size_y, depth), F32),
            VMEM((2 * len(PLUS_Y), size_x, depth), F32),
            VMEM((128, 128), F32),
            dma((2 * len(PLUS_X),)),
            dma((2 * len(PLUS_Y),)),
        ],
        compiler_params=params,
        name="spread",
    )(rotation_init.reshape(1, 3), sums, linear, pack, velocity, density, populations)
    x_low = shifted(x_up, 1, 0)
    x_high = shifted(x_down, -1, 0)
    whole = pl.pallas_call(
        functools.partial(collide_kernel, size_x),
        in_specs=[pl.BlockSpec(memory_space=pl.ANY)] * 3,
        out_specs=pl.BlockSpec(memory_space=pl.ANY),
        out_shape=shape(populations.shape, F32),
        scratch_shapes=[
            held,
            VMEM((size_x, size_y, 3 * depth), F32),
            VMEM((size_x, size_y, depth), F32),
            dma((3, size_x)),
            dma((size_x, Q)),
        ],
        compiler_params=params,
        cost_estimate=pl.CostEstimate(flops=100_000_000, bytes_accessed=20_000_000, transcendentals=0),
        name="collide",
    )(populations, moved, density)
    small = [y_face, y_face, corner, corner, corner, corner]
    y_low, y_high, c7, c8, c9, c10 = pl.pallas_call(
        functools.partial(trade_kernel, count_x, count_y),
        in_specs=[vmem()] * 6 + [pl.BlockSpec(memory_space=pl.ANY)],
        out_specs=[vmem()] * 6,
        out_shape=small,
        scratch_shapes=[VMEM(one.shape, F32) for one in small] + [dma((6,)), dma((6,))],
        compiler_params=pltpu.CompilerParams(collective_id=1, has_side_effects=True),
        cost_estimate=pl.CostEstimate(flops=20_000_000, bytes_accessed=1_000_000, transcendentals=0),
        name="trade",
    )(y_up, y_down, c7, c8, c9, c10, whole)
    whole = pl.pallas_call(
        edge_kernel,
        in_specs=[pl.BlockSpec(memory_space=pl.ANY)] + [vmem()] * 8,
        out_specs=pl.BlockSpec(memory_space=pl.ANY),
        out_shape=shape(populations.shape, F32),
        scratch_shapes=[
            VMEM((2 * len(PLUS_X), size_y, depth), F32),
            VMEM((2 * len(PLUS_Y), size_x, depth), F32),
            dma((2 * len(PLUS_X),)),
            dma((2 * len(PLUS_Y),)),
        ],
        input_output_aliases={0: 0},
        name="edges",
    )(whole, x_low, x_high, y_low, y_high, c7, c8, c9, c10)
    return whole, spins


def solution(mesh):
    return jax.shard_map(
        local,
        mesh=mesh,
        in_specs=(
            P(None, "gx", "gy", None),
            P(),
            P(None, "gx", "gy", None),
            P("gx", "gy"),
            P(None, "gx", "gy", None),
            P("gx", "gy", None),
            P("gx", "gy", None),
        ),
        out_specs=(P(None, "gx", "gy", None), P()),
        check_vma=False,
    )
```

profile of v0, /device:TPU:0, one launch (start us, length us, event | category | flops | bytes accessed | tf_op | source)
XLA Modules:
  0.0 74.6 jit_solution(763740329260471111)
XLA Ops:
  0.6 0.0 copy-start.4
  0.6 0.0 copy-start.2
  0.7 0.0 copy-start.3
  1.3 0.8 %copy.12 = f32[3,1,1,2048]{3,0,1,2:T(4,128)S(1)} copy(f32[3,1,1,2048]{3,2,1,0:T(1,128)} %param.11) | data formatting | bytes 49152
  2.1 5.3 %moments.1 = (f32[512,256]{1,0:T(8,128)}, f32[512,768]{1,0:T(8,128)}) custom-call(f32[19,8,64,256]{3,2,1,0:T(8,128)} %pops_ref.5), custom_call_target="tpu_custom_call" | custom-call | tf_op jit(solution)/shard_map/moments/pallas_call | solution.py:598
  7.4 0.0 copy-done.4
  7.5 0.0 copy-done.2
  7.5 0.0 copy-done.3
  7.5 0.7 concatenate.3.pack_ref
  8.2 20.1 %gather.1 = (f32[8,128]{1,0:T(8,128)}, f32[16,2048]{1,0:T(8,128)}) custom-call(f32[512,768]{1,0:T(8,128)} %get-tuple-element.22.velocity_ref, f32[8,2048]{1,0:T(8,128)} %concatenate.3.pack_ref), custom_call_target="tpu_custom_call" | custom-call | tf_op jit(solution)/shard_map/gather/pallas_call | solution.py:608
  28.3 12.9 %total.1.sums_ref = f32[8,128]{1,0:T(8,128)} custom-call(f32[8,128]{1,0:T(8,128)} %get-tuple-element.23.part_ref), custom_call_target="tpu_custom_call" | custom-call | tf_op jit(solution)/shard_map/total/pallas_call | solution.py:630
  41.3 7.7 %spread.1 = (f32[512,768]{1,0:T(8,128)}, f32[3,3]{1,0:T(4,128)}, f32[5,64,256]{2,1,0:T(8,128)}, f32[5,64,256]{2,1,0:T(8,128)}, f32[5,8,256]{2,1,0:T(8,128)}, /*i...) custom-call(f32[1,3]{1,0:T(1,128)} %bitcast.15, ...), custom_call_target="tpu_custom_call" | custom-call | tf_op jit(solution)/shard_map/spread/pallas_call | solution.py:650
  49.0 1.6 %collective-permute-start = (f32[5,64,256]{2,1,0:T(8,128)}, f32[5,64,256]{2,1,0:T(8,128)S(1)}, u32[]{:S(2)}, u32[]{:S(2)}) collective-permute-start(f32[5,64,256]{2,1,0:T(8,128)} %get-tuple-element.27), channel_id=1, source_target_pairs={{0,4},{1,5},{2,6},{3,7},{4,8},{5,9},{6,10},{7,11},{8,12},{9,13},{1... | collective-permute-start | bytes 983048 | tf_op jit(solution)/shard_map/ppermute | solution.py:571
  50.5 3.2 %collective-permute-start.1 = (f32[5,64,256]{2,1,0:T(8,128)}, f32[5,64,256]{2,1,0:T(8,128)S(1)}, u32[]{:S(2)}, u32[]{:S(2)}) collective-permute-start(f32[5,64,256]{2,1,0:T(8,128)} %get-tuple-element.28), channel_id=1, source_target_pairs={{0,28},{1,29},{2,30},{3,31},{4,0},{5,1},{6,2},{7,3},{8,4},{9,5},{1... | collective-permute-start | bytes 983048 | tf_op jit(solution)/shard_map/ppermute | solution.py:571
  53.8 9.5 %collide.1.refs_6_.whole_ref = f32[19,8,64,256]{3,2,1,0:T(8,128)} custom-call(f32[19,8,64,256]{3,2,1,0:T(8,128)} %pops_ref.5, f32[512,768]{1,0:T(8,128)} %get-tuple-element.26.velocity_ref, f32[512,256]{1,0:T(8,128)} %get-tuple-element.25.density_ref), custom_call_target="tpu_custom_call" | custom-call | flops 100000000 | bytes 20000000 | tf_op jit(solution)/shard_map/collide/pallas_call | solution.py:681
  63.3 8.2 %trade.1 = (f32[5,8,256]{2,1,0:T(8,128)}, f32[5,8,256]{2,1,0:T(8,128)}, f32[1,256]{1,0:T(1,128)}, f32[1,256]{1,0:T(1,128)}, f32[1,256]{1,0:T(1,128)}, /*index=5*/f32[1,256]{1,0:T(1,128)}) custom-call(f32[5,8,256]{2,1,0:T(8,128)} %get-tuple-element.29.refs_0_, f32[5,8,256]{2,1,0:T(8,128)} %get-tuple-element.30.refs_1_, f32[1,256]{1,0:T(1,128)} %get-tuple-element.31.refs_2_, ...), custom_call_target="tpu_custom_call" | custom-call | flops 20000000 | bytes 1000000 | tf_op jit(solution)/shard_map/trade/pallas_call | solution.py:698
  71.5 0.0 collective-permute-done.x_low
  71.5 0.0 copy-start
  71.5 0.0 collective-permute-done.1.x_high
  71.5 0.0 copy-start.1
  71.5 0.7 copy-done
  72.2 0.1 copy-done.1
  72.4 2.3 %edges.1 = f32[19,8,64,256]{3,2,1,0:T(8,128)} custom-call(f32[19,8,64,256]{3,2,1,0:T(8,128)} %collide.1.refs_6_.whole_ref, f32[5,64,256]{2,1,0:T(8,128)} %copy-done, f32[5,64,256]{2,1,0:T(8,128)} %copy-done.1, f32[5,8,256]{2,1,0:T(8,128)} %get-tuple-element.35.y_low, f32[5,8,256]{2,1,0:T(8,128)} %get-tuple-element.36.y_high, ...), custom_call_target="tpu_custom_call", output_to_operand_aliasing={{}: (0, {})} | custom-call | tf_op jit(solution)/shard_map/edges/pallas_call | solution.py:708
  (3 shorter events, 0.0 us)
Async XLA Ops:
  0.6 6.8 %copy-start.4 = (f32[1,1,2048]{2,1,0:T(1,128)S(1)}, f32[1,1,2048]{2,1,0:T(1,128)}, u32[]{:S(2)}) copy-start(f32[1,1,2048]{2,1,0:T(1,128)} %param.12) | copy-start | bytes 24580
  0.6 6.8 %copy-start.2 = (s32[3,1,1,2048]{3,2,1,0:T(1,128)S(1)}, s32[3,1,1,2048]{3,2,1,0:T(1,128)}, u32[]{:S(2)}) copy-start(s32[3,1,1,2048]{3,2,1,0:T(1,128)} %param.9) | copy-start | bytes 73732
  0.7 6.9 %copy-start.3 = (f32[1,1,2048]{2,1,0:T(1,128)S(1)}, f32[1,1,2048]{2,1,0:T(1,128)}, u32[]{:S(2)}) copy-start(f32[1,1,2048]{2,1,0:T(1,128)} %param.13) | copy-start | bytes 24580
  49.0 22.5 %collective-permute-start = (f32[5,64,256]{2,1,0:T(8,128)}, f32[5,64,256]{2,1,0:T(8,128)S(1)}, u32[]{:S(2)}, u32[]{:S(2)}) collective-permute-start(f32[5,64,256]{2,1,0:T(8,128)} %get-tuple-element.27), channel_id=1, source_target_pairs={{0,4},{1,5},{2,6},{3,7},{4,8},{5,9},{6,10},{7,11},{8,12},{9,13},{1... | collective-permute-start | bytes 983048 | tf_op jit(solution)/shard_map/ppermute | solution.py:571
  50.5 21.0 %collective-permute-start.1 = (f32[5,64,256]{2,1,0:T(8,128)}, f32[5,64,256]{2,1,0:T(8,128)S(1)}, u32[]{:S(2)}, u32[]{:S(2)}) collective-permute-start(f32[5,64,256]{2,1,0:T(8,128)} %get-tuple-element.28), channel_id=1, source_target_pairs={{0,28},{1,29},{2,30},{3,31},{4,0},{5,1},{6,2},{7,3},{8,4},{9,5},{1... | collective-permute-start | bytes 983048 | tf_op jit(solution)/shard_map/ppermute | solution.py:571
  71.5 0.7 copy-start
  71.5 0.8 %copy-start.1 = (f32[5,64,256]{2,1,0:T(8,128)}, f32[5,64,256]{2,1,0:T(8,128)S(1)}, u32[]{:S(2)}) copy-start(f32[5,64,256]{2,1,0:T(8,128)S(1)} %collective-permute-done.1.x_high) | copy-start | bytes 983044
where the time goes:
time: 75 us; the launch traced here: 74.6 us
  Pallas kernels  66.1 us (88%)
  starting transfers between devices  4.78 us (6%)
  local copies, waits for them, and re-layouts  2.28 us (3%)
  between operations  1.45 us (2%)
    pallas_call x1, Pallas kernels, local(): pl.pallas_call(gather_kernel, in_specs=[vmem()] * 2, out_specs=[vmem()] *...  20.1 us
    pallas_call x1, Pallas kernels, local(): pl.pallas_call(functools.partial(total_kernel, count_x, count_y), in_spec...  12.9 us
    pallas_call x1, Pallas kernels, local(): pl.pallas_call(functools.partial(collide_kernel, size_x), in_specs=[pl.Bl...  9.51 us
    pallas_call x1, Pallas kernels, local(): pl.pallas_call(functools.partial(trade_kernel, count_x, count_y), in_spec...  8.21 us
    pallas_call x1, Pallas kernels, local(): pl.pallas_call(functools.partial(spread_kernel, size_y), in_specs=[vmem()...  7.73 us
    pallas_call x1, Pallas kernels, local(): pl.pallas_call(moments_kernel, in_specs=[pl.BlockSpec(memory_space=pl.ANY...  5.34 us
    ppermute x2, starting transfers between devices, shifted(): return lax.ppermute(value, ('gx', 'gy'), pairs)  4.78 us
    pallas_call x1, Pallas kernels, local(): pl.pallas_call(edge_kernel, in_specs=[pl.BlockSpec(memory_space=pl.ANY)]...  2.27 us
  transfers between devices with their start and end apart: 2, of which 0 were waited for; matrix products, arithmetic and copies ran while one was open for 0% of the time, Pallas kernels for 24%

commit v1 on v0

v1 whole, which is shorter than its diff:
```python
import functools

import jax
import jax.numpy as jnp
from jax import lax
from jax.experimental import pallas as pl
from jax.experimental.pallas import tpu as pltpu
from jax.sharding import PartitionSpec as P

Q = 19
ITERS = 3
VELOCITY_TABLE = (
    (0, 0, 0),
    (1, 0, 0),
    (-1, 0, 0),
    (0, 1, 0),
    (0, -1, 0),
    (0, 0, 1),
    (0, 0, -1),
    (1, 1, 0),
    (-1, -1, 0),
    (1, -1, 0),
    (-1, 1, 0),
    (1, 0, 1),
    (-1, 0, -1),
    (1, 0, -1),
    (-1, 0, 1),
    (0, 1, 1),
    (0, -1, -1),
    (0, 1, -1),
    (0, -1, 1),
)
WEIGHT_TABLE = (1.0 / 3.0,) + (1.0 / 18.0,) * 6 + (1.0 / 36.0,) * 12
RELAX_TIME = 0.8
SPREAD_GAIN = 0.25
SPIN_GAIN = 0.5
PLUS_X = [m for m in range(Q) if VELOCITY_TABLE[m][0] == 1]
MINUS_X = [m for m in range(Q) if VELOCITY_TABLE[m][0] == -1]
PLUS_Y = [m for m in range(Q) if VELOCITY_TABLE[m][1] == 1]
MINUS_Y = [m for m in range(Q) if VELOCITY_TABLE[m][1] == -1]
MESH = pl.DeviceIdType.MESH
F32 = jnp.float32
BF16 = jnp.bfloat16
VMEM = pltpu.VMEM


def vmem():
    return pl.BlockSpec(memory_space=pltpu.VMEM)


def relax(member, value, density, velocity, common):
    direction = VELOCITY_TABLE[member]
    projected = None
    for number in range(3):
        if direction[number] != 0:
            term = velocity[number] if direction[number] > 0 else -velocity[number]
            projected = term if projected is None else projected + term
    scaled = density * (WEIGHT_TABLE[member] / RELAX_TIME)
    if projected is None:
        bracket = common
    else:
        bracket = common + projected * (3.0 + 4.5 * projected)
    return value * (1.0 - 1.0 / RELAX_TIME) + scaled * bracket


def common_of(velocity):
    squared = velocity[0] * velocity[0] + velocity[1] * velocity[1] + velocity[2] * velocity[2]
    return 1.0 - 1.5 * squared


def roll(value, steps, axis):
    if steps == 0:
        return value
    return pltpu.roll(value, steps % value.shape[axis], axis)


def push(keep, link, value):
    flow = link * (roll(value, -1, 1) - value)
    return keep * value - flow + roll(flow, 1, 1)


def cross(first, second):
    return [
        first[1] * second[2] - first[2] * second[1],
        first[2] * second[0] - first[0] * second[2],
        first[0] * second[1] - first[1] * second[0],
    ]


PAIRS = ((0, 0), (1, 1), (2, 2), (0, 1), (0, 2), (1, 2))


def paired(first, second):
    return [first[a] * second[b] for a, b in PAIRS]


def forced(omega, lift, still):
    found = list(still)
    for k in range(ITERS):
        term = cross(omega[k], lift[ITERS - 1 - k])
        found = [found[b] + term[b] for b in range(3)]
    return found


def wide_omega(omega_ref, depth):
    def one(index):
        value = SPREAD_GAIN * omega_ref[index * 8 : index * 8 + 8, :]
        return jnp.concatenate([value] * (depth // 128), axis=1)

    return [[one(k * 3 + b) for b in range(3)] for k in range(ITERS)]


def split(row):
    hi = row.astype(BF16)
    return hi, (row - hi.astype(F32)).astype(BF16)


def moved(member, value, layer, y_low, y_high):
    step_y = VELOCITY_TABLE[member][1]
    if step_y == 1:
        halo = y_low[PLUS_Y.index(member), pl.ds(layer, 1), :]
        value = jnp.concatenate([halo, value[:-1]], axis=0)
    elif step_y == -1:
        halo = y_high[MINUS_Y.index(member), pl.ds(layer, 1), :]
        value = jnp.concatenate([value[1:], halo], axis=0)
    return roll(value, VELOCITY_TABLE[member][2], 1)


def main_kernel(
    x_count,
    y_count,
    cell_hbm,
    count_hbm,
    arm_hbm,
    area_hbm,
    share_hbm,
    spin_hbm,
    pops_ref,
    density_ref,
    still_ref,
    lift_ref,
    omega_ref,
    x_up_ref,
    x_down_ref,
    y_low_ref,
    y_high_ref,
    held,
    cell,
    arm,
    area,
    share,
    onehot,
    taps,
    field,
    part,
    slots,
    turned,
    tally,
    spin,
    rim,
    halo,
    mark_sem,
    pops_sem,
    send_sem,
    recv_sem,
    rim_send,
    rim_recv,
):
    layers, _, size_y, depth = held.shape
    planes = layers * size_y
    count = area.shape[1]
    x = lax.axis_index("gx")
    y = lax.axis_index("gy")
    me = x * y_count + y
    steps = [(dx, dy) for dx in range(x_count) for dy in range(y_count) if dx or dy]
    others = [(lax.rem(x + dx, x_count), lax.rem(y + dy, y_count)) for dx, dy in steps]
    marks = [
        pltpu.make_async_copy(source, target, mark_sem.at[n])
        for n, (source, target) in enumerate(
            ((cell_hbm, cell), (arm_hbm, arm), (area_hbm, area), (share_hbm, share), (count_hbm, tally), (spin_hbm, spin))
        )
    ]
    for copy in marks:
        copy.start()

    def incoming(layer):
        return pltpu.make_async_copy(pops_ref.at[:, layer], held.at[layer], pops_sem.at[layer])

    for layer in range(layers):
        incoming(layer).start()
    barrier = pltpu.get_barrier_semaphore()
    for other in others:
        pl.semaphore_signal(barrier, inc=1, device_id=other, device_id_type=MESH)
    for copy in marks:
        copy.wait()

    plane = (cell[0] - x * layers) * size_y + cell[1] - y * size_y
    low = cell[2]
    high = jnp.where(low == depth - 1, 0, low + 1)
    live = lax.broadcasted_iota(jnp.int32, (1, count), 1) < tally[0, 0]
    weight = jnp.where(live, area[...], 0.0)
    lever = [arm[b] for b in range(3)]
    heavy = [weight * lever[b] for b in range(3)]
    after = share[...]
    before = 1.0 - after
    inertia_rows = []
    for row in paired(heavy, lever):
        total = row[:, 0:128]
        for n in range(1, count // 128):
            total = total + row[:, n * 128 : (n + 1) * 128]
        inertia_rows.append(total)
    onehot[...] = jnp.where(
        lax.broadcasted_iota(jnp.int32, (planes, count), 0) == plane, 1.0, 0.0
    ).astype(BF16)
    chunk = 512
    scaled = SPREAD_GAIN * weight
    kinds = [(scaled * before, scaled * after), (scaled * before * after, None)]
    kinds += [(heavy[b] * before, heavy[b] * after) for b in range(3)]
    dims = (((1,), (1,)), ((), ()))
    for number, (at_low, at_high) in enumerate(kinds):
        slot = number % 2
        for start in range(0, count, chunk):
            lanes = slice(start, start + chunk)
            ids = lax.broadcasted_iota(jnp.int32, (depth, chunk), 0)
            on_low = ids == low[:, lanes]
            on_high = ids == high[:, lanes]
            value = jnp.where(on_low, at_low[:, lanes], 0.0)
            if at_high is not None:
                value = jnp.where(on_high, at_high[:, lanes], value)
            hi, lo = split(value)
            taps[slot, 0, :, lanes] = hi
            taps[slot, 1, :, lanes] = lo
        table = onehot[...]
        out = lax.dot_general(table, taps[slot, 0], dims, preferred_element_type=F32)
        out = out + lax.dot_general(table, taps[slot, 1], dims, preferred_element_type=F32)
        if number < 2:
            field[number] = out
        else:
            lift_ref[number - 2] = out

    def moments(layer, carry):
        incoming(layer).wait()
        for start in range(0, size_y, 8):
            at = pl.ds(pl.multiple_of(layer * size_y + start, 8), 8)
            values = [held[layer, m, start : start + 8, :] for m in range(Q)]
            density = values[0]
            for m in range(1, Q):
                density = density + values[m]
            density_ref[at, :] = density
            inverse = 1.0 / density
            for number in range(3):
                total = None
                for m in range(Q):
                    direction = VELOCITY_TABLE[m][number]
                    if direction != 0:
                        if total is None:
                            total = values[m]
                        else:
                            total = total + values[m] if direction > 0 else total - values[m]
                still_ref[number, at, :] = total * inverse
        return carry

    lax.fori_loop(0, layers, moments, 0)

    def folded(value):
        total = value[:, 0:128]
        for n in range(1, depth // 128):
            total = total + value[:, n * 128 : (n + 1) * 128]
        part_sum = total[0:8]
        for n in range(1, block // 8):
            part_sum = part_sum + total[n * 8 : n * 8 + 8]
        return part_sum

    block = 32

    def measure(step, totals):
        at = pl.ds(pl.multiple_of(step * block, block), block)
        keep = 1.0 - field[0, at, :]
        link = field[1, at, :]
        lift = [lift_ref[b, at, :] for b in range(3)]
        flow = [still_ref[b, at, :] for b in range(3)]
        lift_next = [push(keep, link, value) for value in lift]
        flow_next = [push(keep, link, value) for value in flow]
        for b in range(3):
            lift_ref[3 + b, at, :] = lift_next[b]
            still_ref[b, at, :] = flow_next[b]
        found = cross(lift, flow) + cross(lift_next, flow) + cross(lift_next, flow_next)
        found += paired(lift, lift) + paired(lift, lift_next)
        return tuple(total + folded(value) for total, value in zip(totals, found))

    zero = jnp.zeros((8, 128), F32)
    totals = lax.fori_loop(0, planes // block, measure, (zero,) * 21)
    rows = [jnp.sum(total, axis=0, keepdims=True) for total in totals] + inertia_rows
    rows.append(jnp.zeros((5, 128), F32))
    column = jnp.sum(jnp.concatenate(rows, axis=0), axis=1, keepdims=True)
    diagonal = lax.broadcasted_iota(jnp.int32, (32, 128), 0) == lax.broadcasted_iota(jnp.int32, (32, 128), 1)
    mine = jnp.sum(jnp.where(diagonal, column, 0.0), axis=0, keepdims=True)
    part[...] = mine
    slots[pl.ds(me, 1), :] = mine
    pl.semaphore_wait(barrier, len(others))

    def sent(n, row):
        return pltpu.make_async_remote_copy(
            src_ref=part,
            dst_ref=slots.at[pl.ds(row, 1)],
            send_sem=send_sem.at[n],
            recv_sem=recv_sem.at[row],
            device_id=others[n],
            device_id_type=MESH,
        )

    for n in range(len(others)):
        sent(n, me).start()

    def settle(at):
        keep = 1.0 - field[0, at, :]
        link = field[1, at, :]
        for b in range(3):
            lift_ref[6 + b, at, :] = push(keep, link, lift_ref[3 + b, at, :])
            still_ref[b, at, :] = push(keep, link, push(keep, link, still_ref[b, at, :]))

    for layer in range(layers):
        for start in (0, size_y - 8):
            settle(slice(layer * size_y + start, layer * size_y + start + 8))
    ways = ((PLUS_Y, size_y - 1, 1), (MINUS_Y, 0, -1))
    for way, (members, row, _) in enumerate(ways):
        def strided(ref, *index):
            return jnp.concatenate(
                [
                    ref[(*index, slice(n * size_y + row, n * size_y + row + 1), slice(None))]
                    for n in range(layers)
                ],
                axis=0,
            )

        for index, m in enumerate(members):
            rim[way, index] = jnp.concatenate([held[n, m, row : row + 1, :] for n in range(layers)], axis=0)
        rim[way, 5] = strided(density_ref)
        for b in range(3):
            rim[way, 6 + b] = strided(still_ref, b)
        for number in range(3 * ITERS):
            rim[way, 9 + number] = strided(lift_ref, number)
    rims = [
        pltpu.make_async_remote_copy(
            src_ref=rim.at[way],
            dst_ref=halo.at[way],
            send_sem=rim_send.at[way],
            recv_sem=rim_recv.at[way],
            device_id=(x, lax.rem(y + dy + y_count, y_count)),
            device_id_type=MESH,
        )
        for way, (_, _, dy) in enumerate(ways)
    ]
    for copy in rims:
        copy.start()
    inner = (size_y - 16) // 2

    def interior(layer, carry):
        for number in range(2):
            start = layer * size_y + 8 + number * inner
            settle(pl.ds(pl.multiple_of(start, 8), inner))
        return carry

    lax.fori_loop(0, layers, interior, 0)
    for n, (dx, dy) in enumerate(steps):
        source = lax.rem(x - dx + x_count, x_count) * y_count + lax.rem(y - dy + y_count, y_count)
        sent(n, source).wait_recv()
    whole = jnp.sum(slots[...], axis=0, keepdims=True)
    turned[...] = jnp.broadcast_to(
        jnp.sum(jnp.where(diagonal, whole, 0.0), axis=1, keepdims=True), (32, 128)
    )

    def number_at(index):
        return jnp.broadcast_to(turned[index : index + 1, :], (8, 128))

    def tensor(start):
        found = [[None] * 3 for _ in range(3)]
        for n, (a, b) in enumerate(PAIRS):
            found[a][b] = found[b][a] = number_at(start + n)
        return found

    def turning(entry, spin):
        trace = entry[0][0] + entry[1][1] + entry[2][2]
        return [
            spin[b] * trace - (entry[0][b] * spin[0] + entry[1][b] * spin[1] + entry[2][b] * spin[2])
            for b in range(3)
        ]

    once, twice, solid = tensor(9), tensor(15), tensor(21)
    inertia = solid[0][0] + solid[1][1] + solid[2][2]
    spins = [[jnp.full((8, 128), spin[b], F32) for b in range(3)]]
    for step in range(ITERS):
        own = turning(solid, spins[step])
        torque = [number_at(step * 3 + b) - own[b] for b in range(3)]
        if step >= 1:
            back = turning(once, spins[step - 1])
            torque = [torque[b] + SPREAD_GAIN * back[b] for b in range(3)]
        if step >= 2:
            back = turning(twice, spins[step - 2])
            torque = [torque[b] + SPREAD_GAIN * back[b] for b in range(3)]
        spins.append([spins[step][b] + SPIN_GAIN * torque[b] / inertia for b in range(3)])
    for step in range(ITERS + 1):
        for b in range(3):
            index = (step * 3 + b) * 8
            omega_ref[index : index + 8, :] = spins[step][b]
    omega = wide_omega(omega_ref, depth)
    for copy in rims:
        copy.wait_recv()
    for way, (members, out) in enumerate(((PLUS_Y, y_low_ref), (MINUS_Y, y_high_ref))):
        lift = [[halo[way, 9 + k * 3 + b] for b in range(3)] for k in range(ITERS)]
        velocity = forced(omega, lift, [halo[way, 6 + b] for b in range(3)])
        density = halo[way, 5]
        common = common_of(velocity)
        for index, m in enumerate(members):
            out[index] = relax(m, halo[way, index], density, velocity, common)
    for members, out, layer in ((PLUS_X, x_up_ref, layers - 1), (MINUS_X, x_down_ref, 0)):
        at = slice(layer * size_y, (layer + 1) * size_y)
        lift = [[lift_ref[k * 3 + b, at, :] for b in range(3)] for k in range(ITERS)]
        tall = [[value[0:1] for value in one] for one in omega]
        velocity = forced(tall, lift, [still_ref[b, at, :] for b in range(3)])
        density = density_ref[at, :]
        common = common_of(velocity)
        for index, m in enumerate(members):
            value = relax(m, held[layer, m], density, velocity, common)
            out[index] = moved(m, value, layer, y_low_ref, y_high_ref)
    for copy in rims:
        copy.wait_send()
    for n in range(len(others)):
        sent(n, me).wait_send()


def collide_kernel(
    pops_ref,
    density_ref,
    still_ref,
    lift_ref,
    omega_ref,
    y_low,
    y_high,
    out_ref,
    spins_ref,
    held,
    in_sems,
    sems,
):
    layers, _, size_y, depth = held.shape

    def incoming(layer):
        return pltpu.make_async_copy(pops_ref.at[:, layer], held.at[layer], in_sems.at[layer])

    for layer in range(layers):
        incoming(layer).start()
    for step in range(ITERS):
        for b in range(3):
            index = ((step + 1) * 3 + b) * 8
            spins_ref[step : step + 1, b : b + 1] = omega_ref[index : index + 1, 0:1]

    def outgoing(layer, action):
        for m in range(Q):
            step = VELOCITY_TABLE[m][0]

            def go(m=m, step=step):
                copy = pltpu.make_async_copy(held.at[layer, m], out_ref.at[m, layer + step], sems.at[layer, m])
                copy.start() if action == "start" else copy.wait()

            if step == 0:
                go()
            elif step == 1:
                pl.when(layer < layers - 1)(go)
            else:
                pl.when(layer > 0)(go)

    omega = wide_omega(omega_ref, depth)
    omega = [[value[0:1] for value in one] for one in omega]

    def one(layer, carry):
        incoming(layer).wait()
        at = pl.ds(pl.multiple_of(layer * size_y, size_y), size_y)
        lift = [[lift_ref[k * 3 + b, at, :] for b in range(3)] for k in range(ITERS)]
        velocity = forced(omega, lift, [still_ref[b, at, :] for b in range(3)])
        density = density_ref[at, :]
        common = common_of(velocity)
        for m in range(Q):
            value = relax(m, held[layer, m], density, velocity, common)
            held[layer, m] = moved(m, value, layer, y_low, y_high)
        outgoing(layer, "start")
        return carry

    lax.fori_loop(0, layers, one, 0)

    def finish(layer, carry):
        outgoing(layer, "wait")
        return carry

    lax.fori_loop(0, layers, finish, 0)


def edge_kernel(whole_ref, x_low, x_high, out_ref, face_sem):
    del whole_ref
    layers = out_ref.shape[1]
    copies = []
    for members, source, layer in ((PLUS_X, x_low, 0), (MINUS_X, x_high, layers - 1)):
        for index, m in enumerate(members):
            copies.append(
                pltpu.make_async_copy(source.at[index], out_ref.at[m, layer], face_sem.at[len(copies)])
            )
            copies[-1].start()
    for copy in copies:
        copy.wait()


def shifted(value, steps_x, steps_y):
    count_x, count_y = lax.axis_size("gx"), lax.axis_size("gy")
    pairs = []
    for x in range(count_x):
        for y in range(count_y):
            target = ((x + steps_x) % count_x) * count_y + (y + steps_y) % count_y
            pairs.append((x * count_y + y, target))
    return lax.ppermute(value, ("gx", "gy"), pairs)


def local(
    populations, rotation_init, slot_cell, slot_count, marker_arm, marker_area, marker_fraction
):
    _, size_x, size_y, depth = populations.shape
    slots = marker_area.shape[2]
    planes = size_x * size_y
    shape = jax.ShapeDtypeStruct
    count_x, count_y = lax.axis_size("gx"), lax.axis_size("gy")
    devices = count_x * count_y
    dma = pltpu.SemaphoreType.DMA
    hbm = pl.BlockSpec(memory_space=pltpu.HBM)
    held = VMEM((size_x, Q, size_y, depth), F32)
    x_face = (len(PLUS_X), size_y, depth)
    y_face = (len(PLUS_Y), size_x, depth)
    density, still, lift, omega, x_up, x_down, y_low, y_high = pl.pallas_call(
        functools.partial(main_kernel, count_x, count_y),
        in_specs=[hbm] * 7,
        out_specs=[vmem()] * 8,
        out_shape=[
            VMEM((planes, depth), F32),
            VMEM((3, planes, depth), F32),
            VMEM((3 * ITERS, planes, depth), F32),
            VMEM((8 * 3 * (ITERS + 1), 128), F32),
            VMEM(x_face, F32),
            VMEM(x_face, F32),
            VMEM(y_face, F32),
            VMEM(y_face, F32),
        ],
        scratch_shapes=[
            held,
            VMEM((3, 1, slots), jnp.int32),
            VMEM((3, 1, slots), F32),
            VMEM((1, slots), F32),
            VMEM((1, slots), F32),
            VMEM((planes, slots), BF16),
            VMEM((2, 2, depth, slots), BF16),
            VMEM((2, planes, depth), F32),
            VMEM((1, 128), F32),
            VMEM((devices, 128), F32),
            VMEM((32, 128), F32),
            pltpu.SMEM((1, 1), jnp.int32),
            pltpu.SMEM((3,), F32),
            VMEM((2, 18, size_x, depth), F32),
            VMEM((2, 18, size_x, depth), F32),
            dma((6,)),
            dma((size_x,)),
            dma((devices,)),
            dma((devices,)),
            dma((2,)),
            dma((2,)),
        ],
        compiler_params=pltpu.CompilerParams(
            collective_id=0, has_side_effects=True, vmem_limit_bytes=50 * 1024 * 1024
        ),
        name="main",
    )(
        slot_cell.reshape(3, 1, slots),
        slot_count,
        marker_arm.reshape(3, 1, slots),
        marker_area.reshape(1, slots),
        marker_fraction.reshape(1, slots),
        rotation_init,
        populations,
    )
    x_low = shifted(x_up, 1, 0)
    x_high = shifted(x_down, -1, 0)
    whole, spins = pl.pallas_call(
        collide_kernel,
        in_specs=[hbm] + [vmem()] * 6,
        out_specs=[hbm, vmem()],
        out_shape=[shape(populations.shape, F32), shape((ITERS, 3), F32)],
        scratch_shapes=[held, dma((size_x,)), dma((size_x, Q))],
        compiler_params=pltpu.CompilerParams(vmem_limit_bytes=47 * 1024 * 1024),
        cost_estimate=pl.CostEstimate(flops=100_000_000, bytes_accessed=20_000_000, transcendentals=0),
        name="collide",
    )(populations, density, still, lift, omega, y_low, y_high)
    whole = pl.pallas_call(
        edge_kernel,
        in_specs=[hbm] + [vmem()] * 2,
        out_specs=hbm,
        out_shape=shape(populations.shape, F32),
        scratch_shapes=[dma((2 * len(PLUS_X),))],
        input_output_aliases={0: 0},
        compiler_params=pltpu.CompilerParams(vmem_limit_bytes=8 * 1024 * 1024),
        name="edges",
    )(whole, x_low, x_high)
    return whole, spins


def solution(mesh):
    return jax.shard_map(
        local,
        mesh=mesh,
        in_specs=(
            P(None, "gx", "gy", None),
            P(),
            P(None, "gx", "gy", None),
            P("gx", "gy"),
            P(None, "gx", "gy", None),
            P("gx", "gy", None),
            P("gx", "gy", None),
        ),
        out_specs=(P(None, "gx", "gy", None), P()),
        check_vma=False,
    )
```

time: 75 us -> 43.4 us (0.58)
  Pallas kernels: 66.1 us -> 33.8 us
  waiting for transfers between devices: 0.01 us -> 3.39 us
  local copies, waits for them, and re-layouts: 2.28 us -> 0 us
    pallas_call x7 -> x3, Pallas kernels: 66.1 us -> 33.8 us  [the longest x1 23.4 us: local(): pl.pallas_call(functools.partial(main_kernel, count_x, count_y), in_specs...]
    ppermute x2, waiting for transfers between devices: 0.01 us -> 3.39 us  [shifted(): return lax.ppermute(value, ('gx', 'gy'), pairs)]
    unnamed x11 -> x0, local copies, waits for them, and re-layouts: 1.58 us -> none
  transfers between devices with their start and end apart: 2 -> 2, of which waited for: 0 -> 2; matrix products, arithmetic and copies ran while one was open for 0% -> 0% of each run, Pallas kernels for 24% -> 22%
where the time goes in v1:
time: 43.4 us; the launch traced here: 43.3 us
  Pallas kernels  33.8 us (78%)
  starting transfers between devices  4.78 us (11%)
  waiting for transfers between devices  3.39 us (8%)
  between operations  1.29 us (3%)
    pallas_call x1, Pallas kernels, local(): pl.pallas_call(functools.partial(main_kernel, count_x, count_y), in_specs...  23.4 us
    pallas_call x1, Pallas kernels, local(): pl.pallas_call(collide_kernel, in_specs=[hbm] + [vmem()] * 6, out_specs=[...  9.52 us
    ppermute x2, starting transfers between devices, shifted(): return lax.ppermute(value, ('gx', 'gy'), pairs)  4.78 us
    ppermute x2, waiting for transfers between devices, shifted(): return lax.ppermute(value, ('gx', 'gy'), pairs)  3.39 us
    pallas_call x1, Pallas kernels, local(): pl.pallas_call(edge_kernel, in_specs=[hbm] + [vmem()] * 2, out_specs=hbm,...  0.91 us
  transfers between devices with their start and end apart: 2, of which 2 were waited for; matrix products, arithmetic and copies ran while one was open for 0% of the time, Pallas kernels for 22%

profile of v1, /device:TPU:0, one launch (start us, length us, event | category | flops | bytes accessed | tf_op | source)
XLA Modules:
  0.0 43.3 jit_solution(6890420949052316164)
XLA Ops:
  1.3 23.4 %main.1 = (f32[512,256]{1,0:T(8,128)S(1)}, f32[3,512,256]{2,1,0:T(8,128)S(1)}, f32[9,512,256]{2,1,0:T(8,128)S(1)}, f32[96,128]{1,0:T(8,128)S(1)}, f32[5,64,256]{...) custom-call(s32[3,1,2048]{2,1,0:T(1,128)} %bitcast.4, ...), custom_call_target="tpu_custom_call" | custom-call | tf_op jit(solution)/shard_map/main/pallas_call | solution.py:536
  24.7 1.5 %collective-permute-start = (f32[5,64,256]{2,1,0:T(8,128)S(1)}, f32[5,64,256]{2,1,0:T(8,128)S(1)}, u32[]{:S(2)}, u32[]{:S(2)}) collective-permute-start(f32[5,64,256]{2,1,0:T(8,128)S(1)} %get-tuple-element.19), channel_id=1, source_target_pairs={{0,4},{1,5},{2,6},{3,7},{4,8},{5,9},{6,10},{7,11},{8,12},{9,13},{1... | collective-permute-start | bytes 983048 | tf_op jit(solution)/shard_map/ppermute | solution.py:519
  26.2 3.3 %collective-permute-start.1 = (f32[5,64,256]{2,1,0:T(8,128)S(1)}, f32[5,64,256]{2,1,0:T(8,128)S(1)}, u32[]{:S(2)}, u32[]{:S(2)}) collective-permute-start(f32[5,64,256]{2,1,0:T(8,128)S(1)} %get-tuple-element.20), channel_id=1, source_target_pairs={{0,28},{1,29},{2,30},{3,31},{4,0},{5,1},{6,2},{7,3},{8,4},{9,5},{1... | collective-permute-start | bytes 983048 | tf_op jit(solution)/shard_map/ppermute | solution.py:519
  29.5 9.5 %collide.1 = (f32[19,8,64,256]{3,2,1,0:T(8,128)}, f32[3,3]{1,0:T(4,128)}) custom-call(f32[19,8,64,256]{3,2,1,0:T(8,128)} %pops_ref.3, f32[512,256]{1,0:T(8,128)S(1)} %get-tuple-element.12.density_ref, f32[3,512,256]{2,1,0:T(8,128)S(1)} %get-tuple-element.13.still_ref, f32[9,512,256]{2,1,0:T(8,128)S(1)} %get-tuple-element.14.lift_ref, ...), custom_call_target="tpu_custom_call" | custom-call | flops 100000000 | bytes 20000000 | tf_op jit(solution)/shard_map/collide/pallas_call | solution.py:588
  39.0 1.2 %collective-permute-done.x_low = f32[5,64,256]{2,1,0:T(8,128)S(1)} collective-permute-done((f32[5,64,256]{2,1,0:T(8,128)S(1)}, f32[5,64,256]{2,1,0:T(8,128)S(1)}, u32[]{:S(2)}, u32[]{:S(2)}) %collective-permute-start) | collective-permute-done | bytes 327712 | tf_op jit(solution)/shard_map/ppermute | solution.py:519
  40.2 2.2 %collective-permute-done.1.x_high = f32[5,64,256]{2,1,0:T(8,128)S(1)} collective-permute-done((f32[5,64,256]{2,1,0:T(8,128)S(1)}, f32[5,64,256]{2,1,0:T(8,128)S(1)}, u32[]{:S(2)}, u32[]{:S(2)}) %collective-permute-start.1) | collective-permute-done | bytes 327712 | tf_op jit(solution)/shard_map/ppermute | solution.py:519
  42.4 0.9 %edges.1 = f32[19,8,64,256]{3,2,1,0:T(8,128)} custom-call(f32[19,8,64,256]{3,2,1,0:T(8,128)} %get-tuple-element.18.whole_ref, f32[5,64,256]{2,1,0:T(8,128)S(1)} %collective-permute-done.x_low, f32[5,64,256]{2,1,0:T(8,128)S(1)} %collective-permute-done.1.x_high), custom_call_target="tpu_custom_call", output_to_operand_aliasing={{}: (0, {})} | custom-call | tf_op jit(solution)/shard_map/edges/pallas_call | solution.py:598
Async XLA Ops:
  24.7 15.5 %collective-permute-start = (f32[5,64,256]{2,1,0:T(8,128)S(1)}, f32[5,64,256]{2,1,0:T(8,128)S(1)}, u32[]{:S(2)}, u32[]{:S(2)}) collective-permute-start(f32[5,64,256]{2,1,0:T(8,128)S(1)} %get-tuple-element.19), channel_id=1, source_target_pairs={{0,4},{1,5},{2,6},{3,7},{4,8},{5,9},{6,10},{7,11},{8,12},{9,13},{1... | collective-permute-start | bytes 983048 | tf_op jit(solution)/shard_map/ppermute | solution.py:519
  26.2 16.2 %collective-permute-start.1 = (f32[5,64,256]{2,1,0:T(8,128)S(1)}, f32[5,64,256]{2,1,0:T(8,128)S(1)}, u32[]{:S(2)}, u32[]{:S(2)}) collective-permute-start(f32[5,64,256]{2,1,0:T(8,128)S(1)} %get-tuple-element.20), channel_id=1, source_target_pairs={{0,28},{1,29},{2,30},{3,31},{4,0},{5,1},{6,2},{7,3},{8,4},{9,5},{1... | collective-permute-start | bytes 983048 | tf_op jit(solution)/shard_map/ppermute | solution.py:519

commit v2 on v1

--- a/solution.py
+++ b/solution.py
@@ -74,9 +74,8 @@
     return pltpu.roll(value, steps % value.shape[axis], axis)
 
 
-def push(keep, link, value):
-    flow = link * (roll(value, -1, 1) - value)
-    return keep * value - flow + roll(flow, 1, 1)
+def push(band, value):
+    return band[0] * value - (band[1] * roll(value, -1, 1) + band[2] * roll(value, 1, 1))
 
 
 def cross(first, second):
@@ -137,6 +136,7 @@
     spin_hbm,
     pops_ref,
     density_ref,
+    field,
     still_ref,
     lift_ref,
     omega_ref,
@@ -151,7 +151,6 @@
     share,
     onehot,
     taps,
-    field,
     part,
     slots,
     turned,
@@ -159,6 +158,9 @@
     spin,
     rim,
     halo,
+    first,
+    face_lift,
+    face_still,
     mark_sem,
     pops_sem,
     send_sem,
@@ -186,17 +188,19 @@
     def incoming(layer):
         return pltpu.make_async_copy(pops_ref.at[:, layer], held.at[layer], pops_sem.at[layer])
 
-    for layer in range(layers):
-        incoming(layer).start()
     barrier = pltpu.get_barrier_semaphore()
     for other in others:
         pl.semaphore_signal(barrier, inc=1, device_id=other, device_id_type=MESH)
     for copy in marks:
         copy.wait()
-
-    plane = (cell[0] - x * layers) * size_y + cell[1] - y * size_y
+    for layer in range(layers):
+        incoming(layer).start()
+
+    plane_x = cell[0] - x * layers
+    plane_y = cell[1] - y * size_y
     low = cell[2]
-    high = jnp.where(low == depth - 1, 0, low + 1)
+    high = jnp.where(low == depth - 1, 0, low + 1).astype(F32).astype(BF16)
+    low = low.astype(F32).astype(BF16)
     live = lax.broadcasted_iota(jnp.int32, (1, count), 1) < tally[0, 0]
     weight = jnp.where(live, area[...], 0.0)
     lever = [arm[b] for b in range(3)]
@@ -209,37 +213,56 @@
         for n in range(1, count // 128):
             total = total + row[:, n * 128 : (n + 1) * 128]
         inertia_rows.append(total)
-    onehot[...] = jnp.where(
-        lax.broadcasted_iota(jnp.int32, (planes, count), 0) == plane, 1.0, 0.0
-    ).astype(BF16)
-    chunk = 512
+    ids = lax.broadcasted_iota(jnp.int32, (size_y, 128), 0).astype(F32).astype(BF16)
+    one = jnp.ones((size_y, 128), BF16)
+    none = jnp.zeros((size_y, 128), BF16)
+    for layer in range(layers):
+        key = jnp.where(plane_x == layer, plane_y, -1).astype(F32).astype(BF16)
+        for start in range(0, count, 128):
+            lanes = slice(start, start + 128)
+            hit = ids == jnp.broadcast_to(key[:, lanes], (size_y, 128))
+            onehot[layer * size_y : (layer + 1) * size_y, lanes] = jnp.where(hit, one, none)
     scaled = SPREAD_GAIN * weight
     kinds = [(scaled * before, scaled * after), (scaled * before * after, None)]
     kinds += [(heavy[b] * before, heavy[b] * after) for b in range(3)]
     dims = (((1,), (1,)), ((), ()))
-    for number, (at_low, at_high) in enumerate(kinds):
+
+    def scattered(number):
+        at_low, at_high = kinds[number]
         slot = number % 2
-        for start in range(0, count, chunk):
-            lanes = slice(start, start + chunk)
-            ids = lax.broadcasted_iota(jnp.int32, (depth, chunk), 0)
-            on_low = ids == low[:, lanes]
-            on_high = ids == high[:, lanes]
-            value = jnp.where(on_low, at_low[:, lanes], 0.0)
-            if at_high is not None:
-                value = jnp.where(on_high, at_high[:, lanes], value)
-            hi, lo = split(value)
-            taps[slot, 0, :, lanes] = hi
-            taps[slot, 1, :, lanes] = lo
+        low_parts = split(at_low)
+        high_parts = None if at_high is None else split(at_high)
+        deep = lax.broadcasted_iota(jnp.int32, (depth, 128), 0).astype(F32).astype(BF16)
+        empty = jnp.zeros((depth, 128), BF16)
+        for start in range(0, count, 128):
+            lanes = slice(start, start + 128)
+
+            def spread(row):
+                return jnp.broadcast_to(row[:, lanes], (depth, 128))
+
+            on_low = deep == spread(low)
+            on_high = deep == spread(high)
+            for piece in range(2):
+                value = empty
+                if at_high is not None:
+                    value = jnp.where(on_high, spread(high_parts[piece]), value)
+                taps[slot, piece, :, lanes] = jnp.where(on_low, spread(low_parts[piece]), value)
         table = onehot[...]
         out = lax.dot_general(table, taps[slot, 0], dims, preferred_element_type=F32)
-        out = out + lax.dot_general(table, taps[slot, 1], dims, preferred_element_type=F32)
-        if number < 2:
-            field[number] = out
-        else:
-            lift_ref[number - 2] = out
+        return out + lax.dot_general(table, taps[slot, 1], dims, preferred_element_type=F32)
+
+    for number in range(2):
+        field[number] = scattered(number)
+    for number in range(3):
+        lift_ref[number] = scattered(2 + number)
 
     def moments(layer, carry):
         incoming(layer).wait()
+        tier = pl.ds(pl.multiple_of(layer * size_y, size_y), size_y)
+        link = field[1, tier, :]
+        back = roll(link, 1, 1)
+        field[0, tier, :] = 1.0 - field[0, tier, :] + (link + back)
+        field[2, tier, :] = back
         for start in range(0, size_y, 8):
             at = pl.ds(pl.multiple_of(layer * size_y + start, 8), 8)
             values = [held[layer, m, start : start + 8, :] for m in range(Q)]
@@ -257,71 +280,11 @@
                             total = values[m]
                         else:
                             total = total + values[m] if direction > 0 else total - values[m]
-                still_ref[number, at, :] = total * inverse
+                first[number, at, :] = total * inverse
         return carry
 
     lax.fori_loop(0, layers, moments, 0)
-
-    def folded(value):
-        total = value[:, 0:128]
-        for n in range(1, depth // 128):
-            total = total + value[:, n * 128 : (n + 1) * 128]
-        part_sum = total[0:8]
-        for n in range(1, block // 8):
-            part_sum = part_sum + total[n * 8 : n * 8 + 8]
-        return part_sum
-
-    block = 32
-
-    def measure(step, totals):
-        at = pl.ds(pl.multiple_of(step * block, block), block)
-        keep = 1.0 - field[0, at, :]
-        link = field[1, at, :]
-        lift = [lift_ref[b, at, :] for b in range(3)]
-        flow = [still_ref[b, at, :] for b in range(3)]
-        lift_next = [push(keep, link, value) for value in lift]
-        flow_next = [push(keep, link, value) for value in flow]
-        for b in range(3):
-            lift_ref[3 + b, at, :] = lift_next[b]
-            still_ref[b, at, :] = flow_next[b]
-        found = cross(lift, flow) + cross(lift_next, flow) + cross(lift_next, flow_next)
-        found += paired(lift, lift) + paired(lift, lift_next)
-        return tuple(total + folded(value) for total, value in zip(totals, found))
-
-    zero = jnp.zeros((8, 128), F32)
-    totals = lax.fori_loop(0, planes // block, measure, (zero,) * 21)
-    rows = [jnp.sum(total, axis=0, keepdims=True) for total in totals] + inertia_rows
-    rows.append(jnp.zeros((5, 128), F32))
-    column = jnp.sum(jnp.concatenate(rows, axis=0), axis=1, keepdims=True)
-    diagonal = lax.broadcasted_iota(jnp.int32, (32, 128), 0) == lax.broadcasted_iota(jnp.int32, (32, 128), 1)
-    mine = jnp.sum(jnp.where(diagonal, column, 0.0), axis=0, keepdims=True)
-    part[...] = mine
-    slots[pl.ds(me, 1), :] = mine
     pl.semaphore_wait(barrier, len(others))
-
-    def sent(n, row):
-        return pltpu.make_async_remote_copy(
-            src_ref=part,
-            dst_ref=slots.at[pl.ds(row, 1)],
-            send_sem=send_sem.at[n],
-            recv_sem=recv_sem.at[row],
-            device_id=others[n],
-            device_id_type=MESH,
-        )
-
-    for n in range(len(others)):
-        sent(n, me).start()
-
-    def settle(at):
-        keep = 1.0 - field[0, at, :]
-        link = field[1, at, :]
-        for b in range(3):
-            lift_ref[6 + b, at, :] = push(keep, link, lift_ref[3 + b, at, :])
-            still_ref[b, at, :] = push(keep, link, push(keep, link, still_ref[b, at, :]))
-
-    for layer in range(layers):
-        for start in (0, size_y - 8):
-            settle(slice(layer * size_y + start, layer * size_y + start + 8))
     ways = ((PLUS_Y, size_y - 1, 1), (MINUS_Y, 0, -1))
     for way, (members, row, _) in enumerate(ways):
         def strided(ref, *index):
@@ -337,9 +300,9 @@
             rim[way, index] = jnp.concatenate([held[n, m, row : row + 1, :] for n in range(layers)], axis=0)
         rim[way, 5] = strided(density_ref)
         for b in range(3):
-            rim[way, 6 + b] = strided(still_ref, b)
-        for number in range(3 * ITERS):
-            rim[way, 9 + number] = strided(lift_ref, number)
+            rim[way, 6 + b] = strided(first, b)
+            rim[way, 9 + b] = strided(lift_ref, b)
+            rim[way, 12 + b] = strided(field, b)
     rims = [
         pltpu.make_async_remote_copy(
             src_ref=rim.at[way],
@@ -353,15 +316,79 @@
     ]
     for copy in rims:
         copy.start()
-    inner = (size_y - 16) // 2
-
-    def interior(layer, carry):
-        for number in range(2):
-            start = layer * size_y + 8 + number * inner
-            settle(pl.ds(pl.multiple_of(start, 8), inner))
-        return carry
-
-    lax.fori_loop(0, layers, interior, 0)
+
+    def folded(value):
+        total = value[:, 0:128]
+        for n in range(1, depth // 128):
+            total = total + value[:, n * 128 : (n + 1) * 128]
+        part_sum = total[0:8]
+        for n in range(1, block // 8):
+            part_sum = part_sum + total[n * 8 : n * 8 + 8]
+        return part_sum
+
+    block = 64
+
+    def measure(step, totals):
+        at = pl.ds(pl.multiple_of(step * block, block), block)
+        band = [field[n, at, :] for n in range(3)]
+        lift = [lift_ref[b, at, :] for b in range(3)]
+        lift_next = [push(band, value) for value in lift]
+        flow = [first[b, at, :] for b in range(3)]
+        flow_next = [push(band, value) for value in flow]
+        for b in range(3):
+            lift_ref[3 + b, at, :] = lift_next[b]
+            still_ref[b, at, :] = flow_next[b]
+        found = cross(lift, flow) + cross(lift, flow_next) + cross(lift_next, flow_next)
+        found += paired(lift, lift) + paired(lift, lift_next)
+        return tuple(total + folded(value) for total, value in zip(totals, found))
+
+    zero = jnp.zeros((8, 128), F32)
+    totals = lax.fori_loop(0, planes // block, measure, (zero,) * 21)
+    rows = [jnp.sum(total, axis=0, keepdims=True) for total in totals] + inertia_rows
+    rows.append(jnp.zeros((5, 128), F32))
+    column = jnp.sum(jnp.concatenate(rows, axis=0), axis=1, keepdims=True)
+    diagonal = lax.broadcasted_iota(jnp.int32, (32, 128), 0) == lax.broadcasted_iota(jnp.int32, (32, 128), 1)
+    mine = jnp.sum(jnp.where(diagonal, column, 0.0), axis=0, keepdims=True)
+    part[...] = mine
+    slots[pl.ds(me, 1), :] = mine
+
+    def sent(n, row):
+        return pltpu.make_async_remote_copy(
+            src_ref=part,
+            dst_ref=slots.at[pl.ds(row, 1)],
+            send_sem=send_sem.at[n],
+            recv_sem=recv_sem.at[row],
+            device_id=others[n],
+            device_id_type=MESH,
+        )
+
+    for n in range(len(others)):
+        sent(n, me).start()
+
+    faces = ((PLUS_X, x_up_ref, layers - 1), (MINUS_X, x_down_ref, 0))
+    for side, (_, _, layer) in enumerate(faces):
+        at = slice(layer * size_y, (layer + 1) * size_y)
+        band = [field[n, at, :] for n in range(3)]
+        for b in range(3):
+            face_lift[side, b] = push(band, lift_ref[3 + b, at, :])
+            face_still[side, b] = push(band, still_ref[b, at, :])
+    for side, (_, _, layer) in enumerate(faces):
+        at = slice(layer * size_y, (layer + 1) * size_y)
+        band = [field[n, at, :] for n in range(3)]
+        for b in range(3):
+            face_still[side, b] = push(band, face_still[side, b])
+    for copy in rims:
+        copy.wait_recv()
+    beyond = []
+    for way in range(2):
+        band = [halo[way, 12 + n] for n in range(3)]
+        flow = [halo[way, 6 + b] for b in range(3)]
+        lift = [[halo[way, 9 + b] for b in range(3)]]
+        for _ in range(2):
+            lift.append([push(band, value) for value in lift[-1]])
+        for _ in range(3):
+            flow = [push(band, value) for value in flow]
+        beyond.append((lift, flow))
     for n, (dx, dy) in enumerate(steps):
         source = lax.rem(x - dx + x_count, x_count) * y_count + lax.rem(y - dy + y_count, y_count)
         sent(n, source).wait_recv()
@@ -404,20 +431,18 @@
             index = (step * 3 + b) * 8
             omega_ref[index : index + 8, :] = spins[step][b]
     omega = wide_omega(omega_ref, depth)
-    for copy in rims:
-        copy.wait_recv()
     for way, (members, out) in enumerate(((PLUS_Y, y_low_ref), (MINUS_Y, y_high_ref))):
-        lift = [[halo[way, 9 + k * 3 + b] for b in range(3)] for k in range(ITERS)]
-        velocity = forced(omega, lift, [halo[way, 6 + b] for b in range(3)])
+        velocity = forced(omega, *beyond[way])
         density = halo[way, 5]
         common = common_of(velocity)
         for index, m in enumerate(members):
             out[index] = relax(m, halo[way, index], density, velocity, common)
-    for members, out, layer in ((PLUS_X, x_up_ref, layers - 1), (MINUS_X, x_down_ref, 0)):
+    tall = [[value[0:1] for value in one] for one in omega]
+    for side, (members, out, layer) in enumerate(faces):
         at = slice(layer * size_y, (layer + 1) * size_y)
-        lift = [[lift_ref[k * 3 + b, at, :] for b in range(3)] for k in range(ITERS)]
-        tall = [[value[0:1] for value in one] for one in omega]
-        velocity = forced(tall, lift, [still_ref[b, at, :] for b in range(3)])
+        lift = [[lift_ref[k * 3 + b, at, :] for b in range(3)] for k in range(2)]
+        lift.append([face_lift[side, b] for b in range(3)])
+        velocity = forced(tall, lift, [face_still[side, b] for b in range(3)])
         density = density_ref[at, :]
         common = common_of(velocity)
         for index, m in enumerate(members):
@@ -432,6 +457,7 @@
 def collide_kernel(
     pops_ref,
     density_ref,
+    field,
     still_ref,
     lift_ref,
     omega_ref,
@@ -440,6 +466,8 @@
     out_ref,
     spins_ref,
     held,
+    speed,
+    lifted,
     in_sems,
     sems,
 ):
@@ -474,10 +502,16 @@
     omega = [[value[0:1] for value in one] for one in omega]
 
     def one(layer, carry):
+        at = pl.ds(pl.multiple_of(layer * size_y, size_y), size_y)
+        band = [field[n, at, :] for n in range(3)]
+        for b in range(3):
+            speed[b] = push(band, still_ref[b, at, :])
+            lifted[b] = push(band, lift_ref[3 + b, at, :])
+        still = [push(band, speed[b]) for b in range(3)]
+        lift = [[lift_ref[k * 3 + b, at, :] for b in range(3)] for k in range(2)]
+        lift.append([lifted[b] for b in range(3)])
+        velocity = forced(omega, lift, still)
         incoming(layer).wait()
-        at = pl.ds(pl.multiple_of(layer * size_y, size_y), size_y)
-        lift = [[lift_ref[k * 3 + b, at, :] for b in range(3)] for k in range(ITERS)]
-        velocity = forced(omega, lift, [still_ref[b, at, :] for b in range(3)])
         density = density_ref[at, :]
         common = common_of(velocity)
         for m in range(Q):
@@ -533,14 +567,15 @@
     held = VMEM((size_x, Q, size_y, depth), F32)
     x_face = (len(PLUS_X), size_y, depth)
     y_face = (len(PLUS_Y), size_x, depth)
-    density, still, lift, omega, x_up, x_down, y_low, y_high = pl.pallas_call(
+    density, field, still, lift, omega, x_up, x_down, y_low, y_high = pl.pallas_call(
         functools.partial(main_kernel, count_x, count_y),
         in_specs=[hbm] * 7,
-        out_specs=[vmem()] * 8,
+        out_specs=[vmem()] * 9,
         out_shape=[
             VMEM((planes, depth), F32),
             VMEM((3, planes, depth), F32),
-            VMEM((3 * ITERS, planes, depth), F32),
+            VMEM((3, planes, depth), F32),
+            VMEM((6, planes, depth), F32),
             VMEM((8 * 3 * (ITERS + 1), 128), F32),
             VMEM(x_face, F32),
             VMEM(x_face, F32),
@@ -555,14 +590,16 @@
             VMEM((1, slots), F32),
             VMEM((planes, slots), BF16),
             VMEM((2, 2, depth, slots), BF16),
-            VMEM((2, planes, depth), F32),
             VMEM((1, 128), F32),
             VMEM((devices, 128), F32),
             VMEM((32, 128), F32),
             pltpu.SMEM((1, 1), jnp.int32),
             pltpu.SMEM((3,), F32),
-            VMEM((2, 18, size_x, depth), F32),
-            VMEM((2, 18, size_x, depth), F32),
+            VMEM((2, 15, size_x, depth), F32),
+            VMEM((2, 15, size_x, depth), F32),
+            VMEM((3, planes, depth), F32),
+            VMEM((2, 3, size_y, depth), F32),
+            VMEM((2, 3, size_y, depth), F32),
             dma((6,)),
             dma((size_x,)),
             dma((devices,)),
@@ -587,14 +624,14 @@
     x_high = shifted(x_down, -1, 0)
     whole, spins = pl.pallas_call(
         collide_kernel,
-        in_specs=[hbm] + [vmem()] * 6,
+        in_specs=[hbm] + [vmem()] * 7,
         out_specs=[hbm, vmem()],
         out_shape=[shape(populations.shape, F32), shape((ITERS, 3), F32)],
-        scratch_shapes=[held, dma((size_x,)), dma((size_x, Q))],
+        scratch_shapes=[held] + [VMEM((3, size_y, depth), F32)] * 2 + [dma((size_x,)), dma((size_x, Q))],
         compiler_params=pltpu.CompilerParams(vmem_limit_bytes=47 * 1024 * 1024),
         cost_estimate=pl.CostEstimate(flops=100_000_000, bytes_accessed=20_000_000, transcendentals=0),
         name="collide",
-    )(populations, density, still, lift, omega, y_low, y_high)
+    )(populations, density, field, still, lift, omega, y_low, y_high)
     whole = pl.pallas_call(
         edge_kernel,
         in_specs=[hbm] + [vmem()] * 2,

time: 43.4 us -> 40.6 us (0.935)
  waiting for transfers between devices: 3.39 us -> 0.47 us
    ppermute x2, waiting for transfers between devices: 3.39 us -> 0.47 us  [shifted(): return lax.ppermute(value, ('gx', 'gy'), pairs)]
    pallas_call x1, Pallas kernels: 23.4 us -> 21.4 us  [local(): pl.pallas_call(functools.partial(main_kernel, count_x, count_y), in_specs...]
    pallas_call x1, Pallas kernels: 9.52 us -> 11.5 us  [local(): pl.pallas_call(collide_kernel, in_specs=[hbm] + [vmem()] * 7, out_specs=[...]
  transfers between devices with their start and end apart: 2 -> 2, of which waited for: 2 -> 1; matrix products, arithmetic and copies ran while one was open for 0% -> 0% of each run, Pallas kernels for 22% -> 29%
where the time goes in v2:
time: 40.6 us; the launch traced here: 40.4 us
  Pallas kernels  33.8 us (83%)
  starting transfers between devices  4.78 us (12%)
  between operations  1.3 us (3%)
  waiting for transfers between devices  0.47 us (1%)
    pallas_call x1, Pallas kernels, local(): pl.pallas_call(functools.partial(main_kernel, count_x, count_y), in_specs...  21.4 us
    pallas_call x1, Pallas kernels, local(): pl.pallas_call(collide_kernel, in_specs=[hbm] + [vmem()] * 7, out_specs=[...  11.5 us
    ppermute x2, starting transfers between devices, shifted(): return lax.ppermute(value, ('gx', 'gy'), pairs)  4.78 us
    pallas_call x1, Pallas kernels, local(): pl.pallas_call(edge_kernel, in_specs=[hbm] + [vmem()] * 2, out_specs=hbm,...  0.91 us
  transfers between devices with their start and end apart: 2, of which 1 were waited for; matrix products, arithmetic and copies ran while one was open for 0% of the time, Pallas kernels for 29%

profile of v2, /device:TPU:0, one launch (start us, length us, event | category | flops | bytes accessed | tf_op | source)
XLA Modules:
  0.0 40.4 jit_solution(11928814307299869805)
XLA Ops:
  1.3 21.4 %main.1 = (f32[512,256]{1,0:T(8,128)S(1)}, f32[3,512,256]{2,1,0:T(8,128)S(1)}, f32[3,512,256]{2,1,0:T(8,128)S(1)}, f32[6,512,256]{2,1,0:T(8,128)S(1)}, f32[96,12...) custom-call(s32[3,1,2048]{2,1,0:T(1,128)} %bitcast.4, ...), custom_call_target="tpu_custom_call" | custom-call | tf_op jit(solution)/shard_map/main/pallas_call | solution.py:570
  22.6 0.6 %collective-permute-start = (f32[5,64,256]{2,1,0:T(8,128)S(1)}, f32[5,64,256]{2,1,0:T(8,128)S(1)}, u32[]{:S(2)}, u32[]{:S(2)}) collective-permute-start(f32[5,64,256]{2,1,0:T(8,128)S(1)} %get-tuple-element.21), channel_id=1, source_target_pairs={{0,4},{1,5},{2,6},{3,7},{4,8},{5,9},{6,10},{7,11},{8,12},{9,13},{1... | collective-permute-start | bytes 983048 | tf_op jit(solution)/shard_map/ppermute | solution.py:553
  23.3 4.2 %collective-permute-start.1 = (f32[5,64,256]{2,1,0:T(8,128)S(1)}, f32[5,64,256]{2,1,0:T(8,128)S(1)}, u32[]{:S(2)}, u32[]{:S(2)}) collective-permute-start(f32[5,64,256]{2,1,0:T(8,128)S(1)} %get-tuple-element.22), channel_id=1, source_target_pairs={{0,28},{1,29},{2,30},{3,31},{4,0},{5,1},{6,2},{7,3},{8,4},{9,5},{1... | collective-permute-start | bytes 983048 | tf_op jit(solution)/shard_map/ppermute | solution.py:553
  27.4 11.5 %collide.1 = (f32[19,8,64,256]{3,2,1,0:T(8,128)}, f32[3,3]{1,0:T(4,128)}) custom-call(f32[19,8,64,256]{3,2,1,0:T(8,128)} %pops_ref.3, f32[512,256]{1,0:T(8,128)S(1)} %get-tuple-element.13.density_ref, f32[3,512,256]{2,1,0:T(8,128)S(1)} %get-tuple-element.14.field, f32[3,512,256]{2,1,0:T(8,128)S(1)} %get-tuple-element.15.still_ref, ...), custom_call_target="tpu_custom_call" | custom-call | flops 100000000 | bytes 20000000 | tf_op jit(solution)/shard_map/collide/pallas_call | solution.py:625
  39.0 0.0 collective-permute-done.x_low
  39.0 0.5 %collective-permute-done.1.x_high = f32[5,64,256]{2,1,0:T(8,128)S(1)} collective-permute-done((f32[5,64,256]{2,1,0:T(8,128)S(1)}, f32[5,64,256]{2,1,0:T(8,128)S(1)}, u32[]{:S(2)}, u32[]{:S(2)}) %collective-permute-start.1) | collective-permute-done | bytes 327712 | tf_op jit(solution)/shard_map/ppermute | solution.py:553
  39.5 0.9 %edges.1 = f32[19,8,64,256]{3,2,1,0:T(8,128)} custom-call(f32[19,8,64,256]{3,2,1,0:T(8,128)} %get-tuple-element.20.whole_ref, f32[5,64,256]{2,1,0:T(8,128)S(1)} %collective-permute-done.x_low, f32[5,64,256]{2,1,0:T(8,128)S(1)} %collective-permute-done.1.x_high), custom_call_target="tpu_custom_call", output_to_operand_aliasing={{}: (0, {})} | custom-call | tf_op jit(solution)/shard_map/edges/pallas_call | solution.py:635
Async XLA Ops:
  22.6 16.3 %collective-permute-start = (f32[5,64,256]{2,1,0:T(8,128)S(1)}, f32[5,64,256]{2,1,0:T(8,128)S(1)}, u32[]{:S(2)}, u32[]{:S(2)}) collective-permute-start(f32[5,64,256]{2,1,0:T(8,128)S(1)} %get-tuple-element.21), channel_id=1, source_target_pairs={{0,4},{1,5},{2,6},{3,7},{4,8},{5,9},{6,10},{7,11},{8,12},{9,13},{1... | collective-permute-start | bytes 983048 | tf_op jit(solution)/shard_map/ppermute | solution.py:553
  23.3 16.2 %collective-permute-start.1 = (f32[5,64,256]{2,1,0:T(8,128)S(1)}, f32[5,64,256]{2,1,0:T(8,128)S(1)}, u32[]{:S(2)}, u32[]{:S(2)}) collective-permute-start(f32[5,64,256]{2,1,0:T(8,128)S(1)} %get-tuple-element.22), channel_id=1, source_target_pairs={{0,28},{1,29},{2,30},{3,31},{4,0},{5,1},{6,2},{7,3},{8,4},{9,5},{1... | collective-permute-start | bytes 983048 | tf_op jit(solution)/shard_map/ppermute | solution.py:553

commit v3 on v2

--- a/solution.py
+++ b/solution.py
@@ -110,8 +110,8 @@
 
 
 def split(row):
-    hi = row.astype(BF16)
-    return hi, (row - hi.astype(F32)).astype(BF16)
+    hi = row.astype(BF16).astype(F32)
+    return hi, (row - hi).astype(BF16).astype(F32)
 
 
 def moved(member, value, layer, y_low, y_high):
@@ -140,8 +140,8 @@
     still_ref,
     lift_ref,
     omega_ref,
-    x_up_ref,
-    x_down_ref,
+    near_ref,
+    far_ref,
     y_low_ref,
     y_high_ref,
     held,
@@ -168,7 +168,7 @@
     rim_send,
     rim_recv,
 ):
-    layers, _, size_y, depth = held.shape
+    _, layers, size_y, depth = held.shape
     planes = layers * size_y
     count = area.shape[1]
     x = lax.axis_index("gx")
@@ -185,22 +185,21 @@
     for copy in marks:
         copy.start()
 
-    def incoming(layer):
-        return pltpu.make_async_copy(pops_ref.at[:, layer], held.at[layer], pops_sem.at[layer])
+    def incoming(half):
+        some = pl.ds(half * (layers // 2), layers // 2)
+        return pltpu.make_async_copy(pops_ref.at[:, some], held.at[:, some], pops_sem.at[half])
 
     barrier = pltpu.get_barrier_semaphore()
     for other in others:
         pl.semaphore_signal(barrier, inc=1, device_id=other, device_id_type=MESH)
     for copy in marks:
         copy.wait()
-    for layer in range(layers):
-        incoming(layer).start()
-
-    plane_x = cell[0] - x * layers
-    plane_y = cell[1] - y * size_y
+    for half in range(2):
+        incoming(half).start()
+
+    plane = (cell[0] - x * layers) * size_y + cell[1] - y * size_y
     low = cell[2]
-    high = jnp.where(low == depth - 1, 0, low + 1).astype(F32).astype(BF16)
-    low = low.astype(F32).astype(BF16)
+    high = jnp.where(low == depth - 1, 0, low + 1)
     live = lax.broadcasted_iota(jnp.int32, (1, count), 1) < tally[0, 0]
     weight = jnp.where(live, area[...], 0.0)
     lever = [arm[b] for b in range(3)]
@@ -213,15 +212,10 @@
         for n in range(1, count // 128):
             total = total + row[:, n * 128 : (n + 1) * 128]
         inertia_rows.append(total)
-    ids = lax.broadcasted_iota(jnp.int32, (size_y, 128), 0).astype(F32).astype(BF16)
-    one = jnp.ones((size_y, 128), BF16)
-    none = jnp.zeros((size_y, 128), BF16)
-    for layer in range(layers):
-        key = jnp.where(plane_x == layer, plane_y, -1).astype(F32).astype(BF16)
-        for start in range(0, count, 128):
-            lanes = slice(start, start + 128)
-            hit = ids == jnp.broadcast_to(key[:, lanes], (size_y, 128))
-            onehot[layer * size_y : (layer + 1) * size_y, lanes] = jnp.where(hit, one, none)
+    for start in range(0, count, 128):
+        lanes = slice(start, start + 128)
+        ids = lax.broadcasted_iota(jnp.int32, (planes, 128), 0)
+        onehot[:, lanes] = jnp.where(ids == plane[:, lanes], 1.0, 0.0)
     scaled = SPREAD_GAIN * weight
     kinds = [(scaled * before, scaled * after), (scaled * before * after, None)]
     kinds += [(heavy[b] * before, heavy[b] * after) for b in range(3)]
@@ -232,21 +226,16 @@
         slot = number % 2
         low_parts = split(at_low)
         high_parts = None if at_high is None else split(at_high)
-        deep = lax.broadcasted_iota(jnp.int32, (depth, 128), 0).astype(F32).astype(BF16)
-        empty = jnp.zeros((depth, 128), BF16)
         for start in range(0, count, 128):
             lanes = slice(start, start + 128)
-
-            def spread(row):
-                return jnp.broadcast_to(row[:, lanes], (depth, 128))
-
-            on_low = deep == spread(low)
-            on_high = deep == spread(high)
+            ids = lax.broadcasted_iota(jnp.int32, (depth, 128), 0)
+            on_low = ids == low[:, lanes]
+            on_high = ids == high[:, lanes]
             for piece in range(2):
-                value = empty
+                value = 0.0
                 if at_high is not None:
-                    value = jnp.where(on_high, spread(high_parts[piece]), value)
-                taps[slot, piece, :, lanes] = jnp.where(on_low, spread(low_parts[piece]), value)
+                    value = jnp.where(on_high, high_parts[piece][:, lanes], value)
+                taps[slot, piece, :, lanes] = jnp.where(on_low, low_parts[piece][:, lanes], value)
         table = onehot[...]
         out = lax.dot_general(table, taps[slot, 0], dims, preferred_element_type=F32)
         return out + lax.dot_general(table, taps[slot, 1], dims, preferred_element_type=F32)
@@ -256,8 +245,17 @@
     for number in range(3):
         lift_ref[number] = scattered(2 + number)
 
+    def advance(tier):
+        band = [field[n, tier, :] for n in range(3)]
+        for b in range(3):
+            still_ref[b, tier, :] = push(band, first[b, tier, :])
+
+    for half in range(2):
+        incoming(half).wait()
+
     def moments(layer, carry):
-        incoming(layer).wait()
+        previous = jnp.maximum(layer - 1, 0)
+        advance(pl.ds(pl.multiple_of(previous * size_y, size_y), size_y))
         tier = pl.ds(pl.multiple_of(layer * size_y, size_y), size_y)
         link = field[1, tier, :]
         back = roll(link, 1, 1)
@@ -265,7 +263,7 @@
         field[2, tier, :] = back
         for start in range(0, size_y, 8):
             at = pl.ds(pl.multiple_of(layer * size_y + start, 8), 8)
-            values = [held[layer, m, start : start + 8, :] for m in range(Q)]
+            values = [held[m, layer, start : start + 8, :] for m in range(Q)]
             density = values[0]
             for m in range(1, Q):
                 density = density + values[m]
@@ -284,6 +282,7 @@
         return carry
 
     lax.fori_loop(0, layers, moments, 0)
+    advance(slice((layers - 1) * size_y, layers * size_y))
     pl.semaphore_wait(barrier, len(others))
     ways = ((PLUS_Y, size_y - 1, 1), (MINUS_Y, 0, -1))
     for way, (members, row, _) in enumerate(ways):
@@ -297,7 +296,7 @@
             )
 
         for index, m in enumerate(members):
-            rim[way, index] = jnp.concatenate([held[n, m, row : row + 1, :] for n in range(layers)], axis=0)
+            rim[way, index] = jnp.concatenate([held[m, n, row : row + 1, :] for n in range(layers)], axis=0)
         rim[way, 5] = strided(density_ref)
         for b in range(3):
             rim[way, 6 + b] = strided(first, b)
@@ -334,10 +333,9 @@
         lift = [lift_ref[b, at, :] for b in range(3)]
         lift_next = [push(band, value) for value in lift]
         flow = [first[b, at, :] for b in range(3)]
-        flow_next = [push(band, value) for value in flow]
+        flow_next = [still_ref[b, at, :] for b in range(3)]
         for b in range(3):
             lift_ref[3 + b, at, :] = lift_next[b]
-            still_ref[b, at, :] = flow_next[b]
         found = cross(lift, flow) + cross(lift, flow_next) + cross(lift_next, flow_next)
         found += paired(lift, lift) + paired(lift, lift_next)
         return tuple(total + folded(value) for total, value in zip(totals, found))
@@ -365,14 +363,14 @@
     for n in range(len(others)):
         sent(n, me).start()
 
-    faces = ((PLUS_X, x_up_ref, layers - 1), (MINUS_X, x_down_ref, 0))
-    for side, (_, _, layer) in enumerate(faces):
+    faces = ((PLUS_X, layers - 1), (MINUS_X, 0))
+    for side, (_, layer) in enumerate(faces):
         at = slice(layer * size_y, (layer + 1) * size_y)
         band = [field[n, at, :] for n in range(3)]
         for b in range(3):
             face_lift[side, b] = push(band, lift_ref[3 + b, at, :])
             face_still[side, b] = push(band, still_ref[b, at, :])
-    for side, (_, _, layer) in enumerate(faces):
+    for side, (_, layer) in enumerate(faces):
         at = slice(layer * size_y, (layer + 1) * size_y)
         band = [field[n, at, :] for n in range(3)]
         for b in range(3):
@@ -438,16 +436,23 @@
         for index, m in enumerate(members):
             out[index] = relax(m, halo[way, index], density, velocity, common)
     tall = [[value[0:1] for value in one] for one in omega]
-    for side, (members, out, layer) in enumerate(faces):
+    even = lax.rem(x, 2) == 0
+    ready = []
+    for side, (members, layer) in enumerate(faces):
         at = slice(layer * size_y, (layer + 1) * size_y)
         lift = [[lift_ref[k * 3 + b, at, :] for b in range(3)] for k in range(2)]
         lift.append([face_lift[side, b] for b in range(3)])
         velocity = forced(tall, lift, [face_still[side, b] for b in range(3)])
-        density = density_ref[at, :]
-        common = common_of(velocity)
-        for index, m in enumerate(members):
-            value = relax(m, held[layer, m], density, velocity, common)
-            out[index] = moved(m, value, layer, y_low_ref, y_high_ref)
+        ready.append((velocity, density_ref[at, :]))
+        ready[-1] += (common_of(velocity),)
+    for index in range(len(PLUS_X)):
+        made = []
+        for (members, layer), (velocity, density, common) in zip(faces, ready):
+            m = members[index]
+            value = relax(m, held[m, layer], density, velocity, common)
+            made.append(moved(m, value, layer, y_low_ref, y_high_ref))
+        near_ref[index] = jnp.where(even, made[0], made[1])
+        far_ref[index] = jnp.where(even, made[1], made[0])
     for copy in rims:
         copy.wait_send()
     for n in range(len(others)):
@@ -529,27 +534,28 @@
     lax.fori_loop(0, layers, finish, 0)
 
 
-def edge_kernel(whole_ref, x_low, x_high, out_ref, face_sem):
+def edge_kernel(whole_ref, near, far, out_ref, face_sem):
     del whole_ref
     layers = out_ref.shape[1]
+    even = 1 - lax.rem(lax.axis_index("gx"), 2)
     copies = []
-    for members, source, layer in ((PLUS_X, x_low, 0), (MINUS_X, x_high, layers - 1)):
-        for index, m in enumerate(members):
-            copies.append(
-                pltpu.make_async_copy(source.at[index], out_ref.at[m, layer], face_sem.at[len(copies)])
-            )
+    for source, upper in ((near, even), (far, 1 - even)):
+        for index, m in enumerate(PLUS_X):
+            member = m + (MINUS_X[index] - m) * upper
+            target = out_ref.at[member, (layers - 1) * upper]
+            copies.append(pltpu.make_async_copy(source.at[index], target, face_sem.at[len(copies)]))
             copies[-1].start()
     for copy in copies:
         copy.wait()
 
 
-def shifted(value, steps_x, steps_y):
+def paired_trade(value, sign):
     count_x, count_y = lax.axis_size("gx"), lax.axis_size("gy")
     pairs = []
     for x in range(count_x):
+        other = (x + (sign if x % 2 == 0 else -sign)) % count_x
         for y in range(count_y):
-            target = ((x + steps_x) % count_x) * count_y + (y + steps_y) % count_y
-            pairs.append((x * count_y + y, target))
+            pairs.append((x * count_y + y, other * count_y + y))
     return lax.ppermute(value, ("gx", "gy"), pairs)
 
 
@@ -567,7 +573,7 @@
     held = VMEM((size_x, Q, size_y, depth), F32)
     x_face = (len(PLUS_X), size_y, depth)
     y_face = (len(PLUS_Y), size_x, depth)
-    density, field, still, lift, omega, x_up, x_down, y_low, y_high = pl.pallas_call(
+    density, field, still, lift, omega, near, far, y_low, y_high = pl.pallas_call(
         functools.partial(main_kernel, count_x, count_y),
         in_specs=[hbm] * 7,
         out_specs=[vmem()] * 9,
@@ -583,13 +589,13 @@
             VMEM(y_face, F32),
         ],
         scratch_shapes=[
-            held,
+            VMEM((Q, size_x, size_y, depth), F32),
             VMEM((3, 1, slots), jnp.int32),
             VMEM((3, 1, slots), F32),
             VMEM((1, slots), F32),
             VMEM((1, slots), F32),
-            VMEM((planes, slots), BF16),
-            VMEM((2, 2, depth, slots), BF16),
+            VMEM((planes, slots), F32),
+            VMEM((2, 2, depth, slots), F32),
             VMEM((1, 128), F32),
             VMEM((devices, 128), F32),
             VMEM((32, 128), F32),
@@ -601,7 +607,7 @@
             VMEM((2, 3, size_y, depth), F32),
             VMEM((2, 3, size_y, depth), F32),
             dma((6,)),
-            dma((size_x,)),
+            dma((2,)),
             dma((devices,)),
             dma((devices,)),
             dma((2,)),
@@ -620,8 +626,8 @@
         rotation_init,
         populations,
     )
-    x_low = shifted(x_up, 1, 0)
-    x_high = shifted(x_down, -1, 0)
+    near = paired_trade(near, 1)
+    far = paired_trade(far, -1)
     whole, spins = pl.pallas_call(
         collide_kernel,
         in_specs=[hbm] + [vmem()] * 7,
@@ -641,7 +647,7 @@
         input_output_aliases={0: 0},
         compiler_params=pltpu.CompilerParams(vmem_limit_bytes=8 * 1024 * 1024),
         name="edges",
-    )(whole, x_low, x_high)
+    )(whole, near, far)
     return whole, spins
 
 

time: 40.6 us -> 39.7 us (0.978)
  starting transfers between devices: 4.78 us -> 2.18 us
  waiting for transfers between devices: 0.47 us -> 2.79 us
  Pallas kernels: 33.8 us -> 33.2 us
    ppermute x2, starting transfers between devices: 4.78 us -> 2.18 us  [paired_trade(): return lax.ppermute(value, ('gx', 'gy'), pairs)]
    ppermute x2, waiting for transfers between devices: 0.47 us -> 2.79 us  [paired_trade(): return lax.ppermute(value, ('gx', 'gy'), pairs)]
    pallas_call x1, Pallas kernels: 21.4 us -> 20.7 us  [local(): pl.pallas_call(functools.partial(main_kernel, count_x, count_y), in_specs...]
where the time goes in v3:
time: 39.7 us; the launch traced here: 39.5 us
  Pallas kernels  33.2 us (84%)
  waiting for transfers between devices  2.79 us (7%)
  starting transfers between devices  2.18 us (5%)
  between operations  1.29 us (3%)
    pallas_call x1, Pallas kernels, local(): pl.pallas_call(functools.partial(main_kernel, count_x, count_y), in_specs...  20.7 us
    pallas_call x1, Pallas kernels, local(): pl.pallas_call(collide_kernel, in_specs=[hbm] + [vmem()] * 7, out_specs=[...  11.5 us
    ppermute x2, waiting for transfers between devices, paired_trade(): return lax.ppermute(value, ('gx', 'gy'), pairs)  2.79 us
    ppermute x2, starting transfers between devices, paired_trade(): return lax.ppermute(value, ('gx', 'gy'), pairs)  2.18 us
    pallas_call x1, Pallas kernels, local(): pl.pallas_call(edge_kernel, in_specs=[hbm] + [vmem()] * 2, out_specs=hbm,...  0.91 us
  transfers between devices with their start and end apart: 2, of which 1 were waited for; matrix products, arithmetic and copies ran while one was open for 0% of the time, Pallas kernels for 29%

profile of v3, /device:TPU:0, one launch (start us, length us, event | category | flops | bytes accessed | tf_op | source)
XLA Modules:
  0.0 39.5 jit_solution(4632164459465665237)
XLA Ops:
  1.3 20.7 %main.1 = (f32[512,256]{1,0:T(8,128)S(1)}, f32[3,512,256]{2,1,0:T(8,128)S(1)}, f32[3,512,256]{2,1,0:T(8,128)S(1)}, f32[6,512,256]{2,1,0:T(8,128)S(1)}, f32[96,12...) custom-call(s32[3,1,2048]{2,1,0:T(1,128)} %bitcast.4, ...), custom_call_target="tpu_custom_call" | custom-call | tf_op jit(solution)/shard_map/main/pallas_call | solution.py:576
  22.0 0.6 %collective-permute-start = (f32[5,64,256]{2,1,0:T(8,128)S(1)}, f32[5,64,256]{2,1,0:T(8,128)S(1)}, u32[]{:S(2)}, u32[]{:S(2)}) collective-permute-start(f32[5,64,256]{2,1,0:T(8,128)S(1)} %get-tuple-element.21), channel_id=1, source_target_pairs={{0,4},{1,5},{2,6},{3,7},{4,0},{5,1},{6,2},{7,3},{8,12},{9,13},{10,... | collective-permute-start | bytes 983048 | tf_op jit(solution)/shard_map/ppermute | solution.py:559
  22.7 1.5 %collective-permute-start.1 = (f32[5,64,256]{2,1,0:T(8,128)S(1)}, f32[5,64,256]{2,1,0:T(8,128)S(1)}, u32[]{:S(2)}, u32[]{:S(2)}) collective-permute-start(f32[5,64,256]{2,1,0:T(8,128)S(1)} %get-tuple-element.22), channel_id=1, source_target_pairs={{0,28},{1,29},{2,30},{3,31},{4,8},{5,9},{6,10},{7,11},{8,4},{9,5},... | collective-permute-start | bytes 983048 | tf_op jit(solution)/shard_map/ppermute | solution.py:559
  24.2 11.5 %collide.1 = (f32[19,8,64,256]{3,2,1,0:T(8,128)}, f32[3,3]{1,0:T(4,128)}) custom-call(f32[19,8,64,256]{3,2,1,0:T(8,128)} %pops_ref.3, f32[512,256]{1,0:T(8,128)S(1)} %get-tuple-element.13.density_ref, f32[3,512,256]{2,1,0:T(8,128)S(1)} %get-tuple-element.14.field, f32[3,512,256]{2,1,0:T(8,128)S(1)} %get-tuple-element.15.still_ref, ...), custom_call_target="tpu_custom_call" | custom-call | flops 100000000 | bytes 20000000 | tf_op jit(solution)/shard_map/collide/pallas_call | solution.py:631
  35.8 2.8 %collective-permute-done.near = f32[5,64,256]{2,1,0:T(8,128)S(1)} collective-permute-done((f32[5,64,256]{2,1,0:T(8,128)S(1)}, f32[5,64,256]{2,1,0:T(8,128)S(1)}, u32[]{:S(2)}, u32[]{:S(2)}) %collective-permute-start) | collective-permute-done | bytes 327712 | tf_op jit(solution)/shard_map/ppermute | solution.py:559
  38.6 0.0 collective-permute-done.1.far
  38.6 0.9 %edges.1 = f32[19,8,64,256]{3,2,1,0:T(8,128)} custom-call(f32[19,8,64,256]{3,2,1,0:T(8,128)} %get-tuple-element.20.whole_ref, f32[5,64,256]{2,1,0:T(8,128)S(1)} %collective-permute-done.near, f32[5,64,256]{2,1,0:T(8,128)S(1)} %collective-permute-done.1.far), custom_call_target="tpu_custom_call", output_to_operand_aliasing={{}: (0, {})} | custom-call | tf_op jit(solution)/shard_map/edges/pallas_call | solution.py:641
Async XLA Ops:
  22.0 16.5 %collective-permute-start = (f32[5,64,256]{2,1,0:T(8,128)S(1)}, f32[5,64,256]{2,1,0:T(8,128)S(1)}, u32[]{:S(2)}, u32[]{:S(2)}) collective-permute-start(f32[5,64,256]{2,1,0:T(8,128)S(1)} %get-tuple-element.21), channel_id=1, source_target_pairs={{0,4},{1,5},{2,6},{3,7},{4,0},{5,1},{6,2},{7,3},{8,12},{9,13},{10,... | collective-permute-start | bytes 983048 | tf_op jit(solution)/shard_map/ppermute | solution.py:559
  22.7 15.9 %collective-permute-start.1 = (f32[5,64,256]{2,1,0:T(8,128)S(1)}, f32[5,64,256]{2,1,0:T(8,128)S(1)}, u32[]{:S(2)}, u32[]{:S(2)}) collective-permute-start(f32[5,64,256]{2,1,0:T(8,128)S(1)} %get-tuple-element.22), channel_id=1, source_target_pairs={{0,28},{1,29},{2,30},{3,31},{4,8},{5,9},{6,10},{7,11},{8,4},{9,5},... | collective-permute-start | bytes 983048 | tf_op jit(solution)/shard_map/ppermute | solution.py:559

commit v4 on v3

--- a/solution.py
+++ b/solution.py
@@ -158,6 +158,8 @@
     spin,
     rim,
     halo,
+    late,
+    late_halo,
     first,
     face_lift,
     face_still,
@@ -252,6 +254,38 @@
 
     for half in range(2):
         incoming(half).wait()
+    pl.semaphore_wait(barrier, len(others))
+    ways = ((PLUS_Y, size_y - 1, 1), (MINUS_Y, 0, -1))
+
+    def strided(ref, row, *index):
+        return jnp.concatenate(
+            [ref[(*index, slice(n * size_y + row, n * size_y + row + 1), slice(None))] for n in range(layers)],
+            axis=0,
+        )
+
+    def carried(source, target, offset):
+        return [
+            pltpu.make_async_remote_copy(
+                src_ref=source.at[way],
+                dst_ref=target.at[way],
+                send_sem=rim_send.at[offset + way],
+                recv_sem=rim_recv.at[offset + way],
+                device_id=(x, lax.rem(y + dy + y_count, y_count)),
+                device_id_type=MESH,
+            )
+            for way, (_, _, dy) in enumerate(ways)
+        ]
+
+    for way, (members, row, _) in enumerate(ways):
+        for index, m in enumerate(members):
+            rim[way, index] = jnp.concatenate([held[m, n, row : row + 1, :] for n in range(layers)], axis=0)
+        for b in range(3):
+            rim[way, 5 + b] = strided(lift_ref, row, b)
+        for n in range(2):
+            rim[way, 8 + n] = strided(field, row, n)
+    rims = carried(rim, halo, 0)
+    for copy in rims:
+        copy.start()
 
     def moments(layer, carry):
         previous = jnp.maximum(layer - 1, 0)
@@ -283,37 +317,12 @@
 
     lax.fori_loop(0, layers, moments, 0)
     advance(slice((layers - 1) * size_y, layers * size_y))
-    pl.semaphore_wait(barrier, len(others))
-    ways = ((PLUS_Y, size_y - 1, 1), (MINUS_Y, 0, -1))
-    for way, (members, row, _) in enumerate(ways):
-        def strided(ref, *index):
-            return jnp.concatenate(
-                [
-                    ref[(*index, slice(n * size_y + row, n * size_y + row + 1), slice(None))]
-                    for n in range(layers)
-                ],
-                axis=0,
-            )
-
-        for index, m in enumerate(members):
-            rim[way, index] = jnp.concatenate([held[m, n, row : row + 1, :] for n in range(layers)], axis=0)
-        rim[way, 5] = strided(density_ref)
-        for b in range(3):
-            rim[way, 6 + b] = strided(first, b)
-            rim[way, 9 + b] = strided(lift_ref, b)
-            rim[way, 12 + b] = strided(field, b)
-    rims = [
-        pltpu.make_async_remote_copy(
-            src_ref=rim.at[way],
-            dst_ref=halo.at[way],
-            send_sem=rim_send.at[way],
-            recv_sem=rim_recv.at[way],
-            device_id=(x, lax.rem(y + dy + y_count, y_count)),
-            device_id_type=MESH,
-        )
-        for way, (_, _, dy) in enumerate(ways)
-    ]
-    for copy in rims:
+    for way, (_, row, _) in enumerate(ways):
+        late[way, 0] = strided(density_ref, row)
+        for b in range(3):
+            late[way, 1 + b] = strided(first, row, b)
+    rims += carried(late, late_halo, 2)
+    for copy in rims[2:]:
         copy.start()
 
     def folded(value):
@@ -379,9 +388,11 @@
         copy.wait_recv()
     beyond = []
     for way in range(2):
-        band = [halo[way, 12 + n] for n in range(3)]
-        flow = [halo[way, 6 + b] for b in range(3)]
-        lift = [[halo[way, 9 + b] for b in range(3)]]
+        link = halo[way, 9]
+        back = roll(link, 1, 1)
+        band = [1.0 - halo[way, 8] + (link + back), link, back]
+        flow = [late_halo[way, 1 + b] for b in range(3)]
+        lift = [[halo[way, 5 + b] for b in range(3)]]
         for _ in range(2):
             lift.append([push(band, value) for value in lift[-1]])
         for _ in range(3):
@@ -431,7 +442,7 @@
     omega = wide_omega(omega_ref, depth)
     for way, (members, out) in enumerate(((PLUS_Y, y_low_ref), (MINUS_Y, y_high_ref))):
         velocity = forced(omega, *beyond[way])
-        density = halo[way, 5]
+        density = late_halo[way, 0]
         common = common_of(velocity)
         for index, m in enumerate(members):
             out[index] = relax(m, halo[way, index], density, velocity, common)
@@ -601,8 +612,10 @@
             VMEM((32, 128), F32),
             pltpu.SMEM((1, 1), jnp.int32),
             pltpu.SMEM((3,), F32),
-            VMEM((2, 15, size_x, depth), F32),
-            VMEM((2, 15, size_x, depth), F32),
+            VMEM((2, 10, size_x, depth), F32),
+            VMEM((2, 10, size_x, depth), F32),
+            VMEM((2, 4, size_x, depth), F32),
+            VMEM((2, 4, size_x, depth), F32),
             VMEM((3, planes, depth), F32),
             VMEM((2, 3, size_y, depth), F32),
             VMEM((2, 3, size_y, depth), F32),
@@ -610,8 +623,8 @@
             dma((2,)),
             dma((devices,)),
             dma((devices,)),
-            dma((2,)),
-            dma((2,)),
+            dma((4,)),
+            dma((4,)),
         ],
         compiler_params=pltpu.CompilerParams(
             collective_id=0, has_side_effects=True, vmem_limit_bytes=50 * 1024 * 1024

time: 39.7 us -> 39.7 us (level)
  no operation moved by 1% of the time
where the time goes in v4:
time: 39.7 us; the launch traced here: 39.5 us
  Pallas kernels  33.2 us (84%)
  waiting for transfers between devices  2.79 us (7%)
  starting transfers between devices  2.18 us (5%)
  between operations  1.29 us (3%)
    pallas_call x1, Pallas kernels, local(): pl.pallas_call(functools.partial(main_kernel, count_x, count_y), in_specs...  20.8 us
    pallas_call x1, Pallas kernels, local(): pl.pallas_call(collide_kernel, in_specs=[hbm] + [vmem()] * 7, out_specs=[...  11.5 us
    ppermute x2, waiting for transfers between devices, paired_trade(): return lax.ppermute(value, ('gx', 'gy'), pairs)  2.79 us
    ppermute x2, starting transfers between devices, paired_trade(): return lax.ppermute(value, ('gx', 'gy'), pairs)  2.18 us
    pallas_call x1, Pallas kernels, local(): pl.pallas_call(edge_kernel, in_specs=[hbm] + [vmem()] * 2, out_specs=hbm,...  0.91 us
  transfers between devices with their start and end apart: 2, of which 1 were waited for; matrix products, arithmetic and copies ran while one was open for 0% of the time, Pallas kernels for 29%

profile of v4, /device:TPU:0, one launch (start us, length us, event | category | flops | bytes accessed | tf_op | source)
XLA Modules:
  0.0 39.5 jit_solution(11209155294629256855)
XLA Ops:
  1.3 20.8 %main.1 = (f32[512,256]{1,0:T(8,128)S(1)}, f32[3,512,256]{2,1,0:T(8,128)S(1)}, f32[3,512,256]{2,1,0:T(8,128)S(1)}, f32[6,512,256]{2,1,0:T(8,128)S(1)}, f32[96,12...) custom-call(s32[3,1,2048]{2,1,0:T(1,128)} %bitcast.4, ...), custom_call_target="tpu_custom_call" | custom-call | tf_op jit(solution)/shard_map/main/pallas_call | solution.py:587
  22.1 0.6 %collective-permute-start = (f32[5,64,256]{2,1,0:T(8,128)S(1)}, f32[5,64,256]{2,1,0:T(8,128)S(1)}, u32[]{:S(2)}, u32[]{:S(2)}) collective-permute-start(f32[5,64,256]{2,1,0:T(8,128)S(1)} %get-tuple-element.21), channel_id=1, source_target_pairs={{0,4},{1,5},{2,6},{3,7},{4,0},{5,1},{6,2},{7,3},{8,12},{9,13},{10,... | collective-permute-start | bytes 983048 | tf_op jit(solution)/shard_map/ppermute | solution.py:570
  22.7 1.5 %collective-permute-start.1 = (f32[5,64,256]{2,1,0:T(8,128)S(1)}, f32[5,64,256]{2,1,0:T(8,128)S(1)}, u32[]{:S(2)}, u32[]{:S(2)}) collective-permute-start(f32[5,64,256]{2,1,0:T(8,128)S(1)} %get-tuple-element.22), channel_id=1, source_target_pairs={{0,28},{1,29},{2,30},{3,31},{4,8},{5,9},{6,10},{7,11},{8,4},{9,5},... | collective-permute-start | bytes 983048 | tf_op jit(solution)/shard_map/ppermute | solution.py:570
  24.2 11.5 %collide.1 = (f32[19,8,64,256]{3,2,1,0:T(8,128)}, f32[3,3]{1,0:T(4,128)}) custom-call(f32[19,8,64,256]{3,2,1,0:T(8,128)} %pops_ref.3, f32[512,256]{1,0:T(8,128)S(1)} %get-tuple-element.13.density_ref, f32[3,512,256]{2,1,0:T(8,128)S(1)} %get-tuple-element.14.field, f32[3,512,256]{2,1,0:T(8,128)S(1)} %get-tuple-element.15.still_ref, ...), custom_call_target="tpu_custom_call" | custom-call | flops 100000000 | bytes 20000000 | tf_op jit(solution)/shard_map/collide/pallas_call | solution.py:644
  35.8 2.8 %collective-permute-done.near = f32[5,64,256]{2,1,0:T(8,128)S(1)} collective-permute-done((f32[5,64,256]{2,1,0:T(8,128)S(1)}, f32[5,64,256]{2,1,0:T(8,128)S(1)}, u32[]{:S(2)}, u32[]{:S(2)}) %collective-permute-start) | collective-permute-done | bytes 327712 | tf_op jit(solution)/shard_map/ppermute | solution.py:570
  38.6 0.0 collective-permute-done.1.far
  38.6 0.9 %edges.1 = f32[19,8,64,256]{3,2,1,0:T(8,128)} custom-call(f32[19,8,64,256]{3,2,1,0:T(8,128)} %get-tuple-element.20.whole_ref, f32[5,64,256]{2,1,0:T(8,128)S(1)} %collective-permute-done.near, f32[5,64,256]{2,1,0:T(8,128)S(1)} %collective-permute-done.1.far), custom_call_target="tpu_custom_call", output_to_operand_aliasing={{}: (0, {})} | custom-call | tf_op jit(solution)/shard_map/edges/pallas_call | solution.py:654
Async XLA Ops:
  22.1 16.5 %collective-permute-start = (f32[5,64,256]{2,1,0:T(8,128)S(1)}, f32[5,64,256]{2,1,0:T(8,128)S(1)}, u32[]{:S(2)}, u32[]{:S(2)}) collective-permute-start(f32[5,64,256]{2,1,0:T(8,128)S(1)} %get-tuple-element.21), channel_id=1, source_target_pairs={{0,4},{1,5},{2,6},{3,7},{4,0},{5,1},{6,2},{7,3},{8,12},{9,13},{10,... | collective-permute-start | bytes 983048 | tf_op jit(solution)/shard_map/ppermute | solution.py:570
  22.7 15.9 %collective-permute-start.1 = (f32[5,64,256]{2,1,0:T(8,128)S(1)}, f32[5,64,256]{2,1,0:T(8,128)S(1)}, u32[]{:S(2)}, u32[]{:S(2)}) collective-permute-start(f32[5,64,256]{2,1,0:T(8,128)S(1)} %get-tuple-element.22), channel_id=1, source_target_pairs={{0,28},{1,29},{2,30},{3,31},{4,8},{5,9},{6,10},{7,11},{8,4},{9,5},... | collective-permute-start | bytes 983048 | tf_op jit(solution)/shard_map/ppermute | solution.py:570

commit v5 on v4

--- a/solution.py
+++ b/solution.py
@@ -545,17 +545,17 @@
     lax.fori_loop(0, layers, finish, 0)
 
 
-def edge_kernel(whole_ref, near, far, out_ref, face_sem):
+def edge_kernel(flip, whole_ref, source, out_ref, face_sem):
     del whole_ref
     layers = out_ref.shape[1]
     even = 1 - lax.rem(lax.axis_index("gx"), 2)
+    upper = 1 - even if flip else even
     copies = []
-    for source, upper in ((near, even), (far, 1 - even)):
-        for index, m in enumerate(PLUS_X):
-            member = m + (MINUS_X[index] - m) * upper
-            target = out_ref.at[member, (layers - 1) * upper]
-            copies.append(pltpu.make_async_copy(source.at[index], target, face_sem.at[len(copies)]))
-            copies[-1].start()
+    for index, m in enumerate(PLUS_X):
+        member = m + (MINUS_X[index] - m) * upper
+        target = out_ref.at[member, (layers - 1) * upper]
+        copies.append(pltpu.make_async_copy(source.at[index], target, face_sem.at[index]))
+        copies[-1].start()
     for copy in copies:
         copy.wait()
 
@@ -651,16 +651,17 @@
         cost_estimate=pl.CostEstimate(flops=100_000_000, bytes_accessed=20_000_000, transcendentals=0),
         name="collide",
     )(populations, density, field, still, lift, omega, y_low, y_high)
-    whole = pl.pallas_call(
-        edge_kernel,
-        in_specs=[hbm] + [vmem()] * 2,
-        out_specs=hbm,
-        out_shape=shape(populations.shape, F32),
-        scratch_shapes=[dma((2 * len(PLUS_X),))],
-        input_output_aliases={0: 0},
-        compiler_params=pltpu.CompilerParams(vmem_limit_bytes=8 * 1024 * 1024),
-        name="edges",
-    )(whole, near, far)
+    for flip, source in ((True, far), (False, near)):
+        whole = pl.pallas_call(
+            functools.partial(edge_kernel, flip),
+            in_specs=[hbm, vmem()],
+            out_specs=hbm,
+            out_shape=shape(populations.shape, F32),
+            scratch_shapes=[dma((len(PLUS_X),))],
+            input_output_aliases={0: 0},
+            compiler_params=pltpu.CompilerParams(vmem_limit_bytes=8 * 1024 * 1024),
+            name="edges_far" if flip else "edges_near",
+        )(whole, source)
     return whole, spins
 
 

time: 39.7 us -> 39.8 us (level)
  Pallas kernels: 33.2 us -> 33.9 us
  waiting for transfers between devices: 2.79 us -> 2.35 us
    pallas_call x1 -> x2, Pallas kernels: 0.91 us -> 1.53 us  [local(): pl.pallas_call(functools.partial(edge_kernel, flip), in_specs=[hbm, vmem(...]
    ppermute x2, waiting for transfers between devices: 2.79 us -> 2.35 us  [paired_trade(): return lax.ppermute(value, ('gx', 'gy'), pairs)]
  transfers between devices with their start and end apart: 2 -> 2, of which waited for: 1 -> 1; matrix products, arithmetic and copies ran while one was open for 0% -> 0% of each run, Pallas kernels for 29% -> 31%
where the time goes in v5:
time: 39.8 us; the launch traced here: 39.6 us
  Pallas kernels  33.9 us (85%)
  waiting for transfers between devices  2.35 us (6%)
  starting transfers between devices  2.11 us (5%)
  between operations  1.31 us (3%)
    pallas_call x1, Pallas kernels, local(): pl.pallas_call(functools.partial(main_kernel, count_x, count_y), in_specs...  20.8 us
    pallas_call x1, Pallas kernels, local(): pl.pallas_call(collide_kernel, in_specs=[hbm] + [vmem()] * 7, out_specs=[...  11.5 us
    ppermute x2, waiting for transfers between devices, paired_trade(): return lax.ppermute(value, ('gx', 'gy'), pairs)  2.35 us
    ppermute x2, starting transfers between devices, paired_trade(): return lax.ppermute(value, ('gx', 'gy'), pairs)  2.11 us
    pallas_call x2, Pallas kernels, local(): pl.pallas_call(functools.partial(edge_kernel, flip), in_specs=[hbm, vmem(...  1.53 us
  transfers between devices with their start and end apart: 2, of which 1 were waited for; matrix products, arithmetic and copies ran while one was open for 0% of the time, Pallas kernels for 31%

profile of v5, /device:TPU:0, one launch (start us, length us, event | category | flops | bytes accessed | tf_op | source)
XLA Modules:
  0.0 39.6 jit_solution(3464410861376976024)
XLA Ops:
  1.3 20.8 %main.1 = (f32[512,256]{1,0:T(8,128)S(1)}, f32[3,512,256]{2,1,0:T(8,128)S(1)}, f32[3,512,256]{2,1,0:T(8,128)S(1)}, f32[6,512,256]{2,1,0:T(8,128)S(1)}, f32[96,12...) custom-call(s32[3,1,2048]{2,1,0:T(1,128)} %bitcast.4, ...), custom_call_target="tpu_custom_call" | custom-call | tf_op jit(solution)/shard_map/main/pallas_call | solution.py:587
  22.1 0.6 %collective-permute-start = (f32[5,64,256]{2,1,0:T(8,128)S(1)}, f32[5,64,256]{2,1,0:T(8,128)S(1)}, u32[]{:S(2)}, u32[]{:S(2)}) collective-permute-start(f32[5,64,256]{2,1,0:T(8,128)S(1)} %get-tuple-element.21), channel_id=1, source_target_pairs={{0,28},{1,29},{2,30},{3,31},{4,8},{5,9},{6,10},{7,11},{8,4},{9,5},... | collective-permute-start | bytes 983048 | tf_op jit(solution)/shard_map/ppermute | solution.py:570
  22.7 1.5 %collective-permute-start.1 = (f32[5,64,256]{2,1,0:T(8,128)S(1)}, f32[5,64,256]{2,1,0:T(8,128)S(1)}, u32[]{:S(2)}, u32[]{:S(2)}) collective-permute-start(f32[5,64,256]{2,1,0:T(8,128)S(1)} %get-tuple-element.22), channel_id=1, source_target_pairs={{0,4},{1,5},{2,6},{3,7},{4,0},{5,1},{6,2},{7,3},{8,12},{9,13},{10,... | collective-permute-start | bytes 983048 | tf_op jit(solution)/shard_map/ppermute | solution.py:570
  24.2 11.5 %collide.1 = (f32[19,8,64,256]{3,2,1,0:T(8,128)}, f32[3,3]{1,0:T(4,128)}) custom-call(f32[19,8,64,256]{3,2,1,0:T(8,128)} %pops_ref.3, f32[512,256]{1,0:T(8,128)S(1)} %get-tuple-element.13.density_ref, f32[3,512,256]{2,1,0:T(8,128)S(1)} %get-tuple-element.14.field, f32[3,512,256]{2,1,0:T(8,128)S(1)} %get-tuple-element.15.still_ref, ...), custom_call_target="tpu_custom_call" | custom-call | flops 100000000 | bytes 20000000 | tf_op jit(solution)/shard_map/collide/pallas_call | solution.py:644
  35.7 0.0 collective-permute-done.source
  35.7 0.8 %edges_far.1.whole_ref = f32[19,8,64,256]{3,2,1,0:T(8,128)} custom-call(f32[19,8,64,256]{3,2,1,0:T(8,128)} %get-tuple-element.20.whole_ref, f32[5,64,256]{2,1,0:T(8,128)S(1)} %collective-permute-done.source), custom_call_target="tpu_custom_call", output_to_operand_aliasing={{}: (0, {})} | custom-call | tf_op jit(solution)/shard_map/edges_far/pallas_call | solution.py:655
  36.5 2.4 %collective-permute-done.1.source = f32[5,64,256]{2,1,0:T(8,128)S(1)} collective-permute-done((f32[5,64,256]{2,1,0:T(8,128)S(1)}, f32[5,64,256]{2,1,0:T(8,128)S(1)}, u32[]{:S(2)}, u32[]{:S(2)}) %collective-permute-start.1) | collective-permute-done | bytes 327712 | tf_op jit(solution)/shard_map/ppermute | solution.py:570
  38.9 0.8 %edges_near.1 = f32[19,8,64,256]{3,2,1,0:T(8,128)} custom-call(f32[19,8,64,256]{3,2,1,0:T(8,128)} %edges_far.1.whole_ref, f32[5,64,256]{2,1,0:T(8,128)S(1)} %collective-permute-done.1.source), custom_call_target="tpu_custom_call", output_to_operand_aliasing={{}: (0, {})} | custom-call | tf_op jit(solution)/shard_map/edges_near/pallas_call | solution.py:655
Async XLA Ops:
  22.1 13.7 %collective-permute-start = (f32[5,64,256]{2,1,0:T(8,128)S(1)}, f32[5,64,256]{2,1,0:T(8,128)S(1)}, u32[]{:S(2)}, u32[]{:S(2)}) collective-permute-start(f32[5,64,256]{2,1,0:T(8,128)S(1)} %get-tuple-element.21), channel_id=1, source_target_pairs={{0,28},{1,29},{2,30},{3,31},{4,8},{5,9},{6,10},{7,11},{8,4},{9,5},... | collective-permute-start | bytes 983048 | tf_op jit(solution)/shard_map/ppermute | solution.py:570
  22.7 16.2 %collective-permute-start.1 = (f32[5,64,256]{2,1,0:T(8,128)S(1)}, f32[5,64,256]{2,1,0:T(8,128)S(1)}, u32[]{:S(2)}, u32[]{:S(2)}) collective-permute-start(f32[5,64,256]{2,1,0:T(8,128)S(1)} %get-tuple-element.22), channel_id=1, source_target_pairs={{0,4},{1,5},{2,6},{3,7},{4,0},{5,1},{6,2},{7,3},{8,12},{9,13},{10,... | collective-permute-start | bytes 983048 | tf_op jit(solution)/shard_map/ppermute | solution.py:570
